TPU v7x, 32 devices: a whole 2x2x4 slice. The times are simulated.
32 devices in a mesh: section: 2 (over x), dp: 16 (over z, y, core).
Axes of the slice: x: 2, y: 2, z: 4, core: 2. Of those that a mesh axis runs over, the one named last changes fastest.
Arguments:
- activations: bfloat16 [4, 256, 4608], P('section', 'dp'), may hold values from -6 to 6
- section_sources: int32 [4], replicated, may hold values from 0 to 3, as said below
- accumulators: float32 [256, 4, 4608], P('dp', 'section'), may hold values from -6 to 6
- block_sources: int32 [256], replicated, may hold values from 0 to 255, as said below
- loss_terms: float32 [2, 16], P('section', 'dp'), may hold values from 0.35 to 6
- pre_gain: float32 [2, 4608], P('section'), may hold values from 0.1 to 1.9
- query_weight: bfloat16 [2, 4608, 2048], P('section', None, 'dp'), may hold values from -0.09375 to 0.09375
- keyval_weight: bfloat16 [2, 4608, 2048], P('section', None, 'dp'), may hold values from -0.09375 to 0.09375
- output_weight: bfloat16 [2, 2048, 4608], P('section', 'dp'), may hold values from -0.125 to 0.125
- post_gain: float32 [2, 4608], P('section'), may hold values from 0.1 to 1.9
Outputs:
- new_activations: bfloat16 [4, 256, 4608], P('section', 'dp')
- new_accumulators: float32 [256, 4, 4608], P('dp', 'section')
- check_out: bfloat16 [2, 256, 4608], P('section', 'dp')
Inputs may be any that keep to these rules, and one draw needn't show every extreme that they name: `section_sources`: A permutation; each old section's micro-batches fill 1 slots of each new section. `block_sources`: A permutation; each old data index's blocks fill 1 block of each new data index.
All inputs are finite; a program needn't handle non-finite values.
Results may differ from a plain program's by a relative error of at most 0.014.
Values may be sent and summed in bfloat16 or wider, within the bound.
No kernel may reach another device: no remote copies, remote signals or barrier semaphores. Data moves between devices by JAX's collectives and lax.ppermute only.
A program may use at most 64 MiB of HBM per device.

v0:
```python
import jax
import jax.numpy as jnp
from jax import lax
from jax.experimental import pallas as pl
from jax.experimental.pallas import tpu as pltpu
from jax.sharding import PartitionSpec as P


def swap(value, axis, mask):
    pairs = [(source, source ^ mask) for source in range(lax.axis_size(axis))]
    return lax.ppermute(value, axis, pairs)


def rms_norm(values, gain):
    meansq = jnp.mean(values * values, axis=-1, keepdims=True)
    return values * lax.rsqrt(meansq + 1e-06) * gain


def rotary(values, positions):
    width = values.shape[-1]
    middle = width // 2
    counter = jnp.arange(middle, dtype=jnp.float32)
    freqs = 10000.0 ** (-2.0 * counter / width)
    angles = positions.astype(jnp.float32)[:, None] * freqs[None, :]
    cosine = jnp.cos(angles)
    sine = jnp.sin(angles)
    first = values[..., :middle]
    second = values[..., middle:]
    return jnp.concatenate(
        [first * cosine - second * sine, second * cosine + first * sine], axis=-1
    )


def place_for(table, peer, own, groups):
    def look(j, place):
        entry = table[peer * groups + j]
        return place + jnp.where(entry // groups == own, entry % groups, 0)

    return lax.fori_loop(0, groups, look, jnp.int32(0), unroll=True)


def pick_sends(sources, section, items):
    groups = items.shape[0]

    def body(table, own_ref, held, out, sem):
        own = own_ref[0]
        copies = []
        for mask in range(1, groups):
            place = place_for(table, own ^ mask, own, groups)
            copies.append(pltpu.make_async_copy(held.at[place], out.at[mask - 1], sem.at[mask - 1]))
            copies[-1].start()
        for copy in copies:
            copy.wait()

    return pl.pallas_call(
        body,
        out_shape=jax.ShapeDtypeStruct((groups - 1,) + items.shape[1:], items.dtype),
        in_specs=[
            pl.BlockSpec(memory_space=pltpu.SMEM),
            pl.BlockSpec(memory_space=pltpu.SMEM),
            pl.BlockSpec(memory_space=pl.ANY),
        ],
        out_specs=pl.BlockSpec(memory_space=pltpu.VMEM),
        scratch_shapes=[pltpu.SemaphoreType.DMA((groups - 1,))],
        name="pick_sends",
    )(sources, section[None], items)


def pack_blocks(sources, rank, blocks, term):
    groups, rows, width = blocks.shape

    def body(table, own_ref, held, term_ref, out):
        own = own_ref[0]
        value = jnp.full((rows, 128), term_ref[0, 0], jnp.float32)
        coarse = value.astype(jnp.bfloat16)
        fine = (value - coarse.astype(jnp.float32)).astype(jnp.bfloat16)
        row = lax.broadcasted_iota(jnp.int32, (rows, 128), 0)
        tail = jnp.where(
            row == 0, coarse.astype(jnp.float32), jnp.where(row == 1, fine.astype(jnp.float32), 0.0)
        ).astype(jnp.bfloat16)

        def one(peer, carry):
            place = place_for(table, peer, own, groups)
            out[peer, :, :width] = held[place].astype(jnp.bfloat16)
            out[peer, :, width:] = tail
            return carry

        lax.fori_loop(0, groups, one, 0)

    return pl.pallas_call(
        body,
        out_shape=jax.ShapeDtypeStruct((groups, rows, width + 128), jnp.bfloat16),
        in_specs=[
            pl.BlockSpec(memory_space=pltpu.SMEM),
            pl.BlockSpec(memory_space=pltpu.SMEM),
            pl.BlockSpec(memory_space=pltpu.VMEM),
            pl.BlockSpec(memory_space=pltpu.SMEM),
        ],
        out_specs=pl.BlockSpec(memory_space=pltpu.VMEM),
        name="pack_blocks",
    )(sources, rank[None], blocks, term)


def place_blocks(sources, rank, blocks):
    groups, rows, width = blocks.shape
    width -= 128

    def body(table, own_ref, held, out):
        own = own_ref[0]

        def add(peer, total):
            return total + held[peer, :, width:].astype(jnp.float32)

        total = lax.fori_loop(0, groups, add, jnp.zeros((rows, 128), jnp.float32))
        factor = groups / jnp.sum(total, axis=0, keepdims=True)[:, :1]

        def one(slot, carry):
            owner = table[own * groups + slot] // groups
            out[slot] = held[owner, :, :width].astype(jnp.float32) * factor
            return carry

        lax.fori_loop(0, groups, one, 0)

    return pl.pallas_call(
        body,
        out_shape=jax.ShapeDtypeStruct((groups, rows, width), jnp.float32),
        in_specs=[
            pl.BlockSpec(memory_space=pltpu.SMEM),
            pl.BlockSpec(memory_space=pltpu.SMEM),
            pl.BlockSpec(memory_space=pltpu.VMEM),
        ],
        out_specs=pl.BlockSpec(memory_space=pltpu.VMEM),
        name="place_blocks",
    )(sources, rank[None], blocks)


def span(masks):
    order = [0]
    for mask in masks:
        order = order + [entry ^ mask for entry in order]
    return order


def step(
    activations,
    section_sources,
    accumulators,
    block_sources,
    loss_terms,
    pre_gain,
    query_weight,
    keyval_weight,
    output_weight,
    post_gain,
):
    sections = lax.axis_size("section")
    section = lax.axis_index("section")
    ranks = lax.axis_size("dp")
    rank = lax.axis_index("dp")
    tokens, width = activations.shape[1:]
    head = query_weight.shape[2]
    assert activations.shape[0] == sections and accumulators.shape[0] == ranks
    assert ranks & (ranks - 1) == 0 and sections & (sections - 1) == 0 and ranks >= 4

    sends = pick_sends(section_sources, section, activations)
    table = section_sources.reshape(sections, sections)
    mine = lax.dynamic_slice_in_dim(table, section, 1, 0)[0]
    mb_from = mine // sections
    kept = jnp.sum(jnp.where(mb_from == section, mine % sections, 0))
    arrived = [lax.dynamic_index_in_dim(activations, kept, 0, keepdims=False)]
    for mask in range(1, sections):
        arrived.append(swap(sends[mask - 1], "section", mask))
    outgoing = pack_blocks(block_sources, rank, accumulators, loss_terms)
    incoming = lax.all_to_all(outgoing, "dp", split_axis=0, concat_axis=0, tiled=True)

    def slot(j):
        value = arrived[0]
        for mask in range(1, sections):
            value = jnp.where(mb_from[j] == (section ^ mask), arrived[mask], value)
        return value

    checked = slot(0)
    moved = jnp.stack([checked] + [slot(j) for j in range(1, sections)])

    wq_other = swap(query_weight[0], "dp", 1)
    wkv_other = swap(keyval_weight[0], "dp", 1)
    wo_other = swap(output_weight[0], "dp", 1)
    weights = jnp.concatenate(
        [query_weight[0], keyval_weight[0], wq_other, wkv_other], axis=1
    )

    rest = [2**b for b in range(1, ranks.bit_length() - 1)]
    top = [rest[-1] | rest[-2]] if len(rest) > 1 else rest
    rest = rest[:-1] if len(rest) > 1 else []
    orders = [top + rest, top + rest[::-1]]
    normed = rms_norm(checked.astype(jnp.float32), pre_gain[0]).astype(jnp.bfloat16)
    cut = width // 256 * 128
    columns = [(0, cut), (cut, width)]
    layout = span(orders[0])
    parts = [normed[None, :, a:b] for a, b in columns]
    for stage in range(len(orders[0])):
        sent = [swap(part, "dp", order[stage]) for part, order in zip(parts, orders)]
        if stage == 1:
            weights, sent = lax.optimization_barrier((weights, sent))
        parts = [jnp.concatenate([part, got]) for part, got in zip(parts, sent)]
    rows = []
    for part, order in zip(parts, orders):
        have = span(order)
        if have != layout:
            part = jnp.concatenate([part[have.index(m)][None] for m in layout])
        rows.append(part.reshape(-1, part.shape[-1]))
    half = rows[0].shape[0]

    proj = sum(
        jnp.dot(part, weights[a:b], preferred_element_type=jnp.float32)
        for part, (a, b) in zip(rows, columns)
    )
    own_at = (rank ^ jnp.array(layout, dtype=jnp.int32)) * tokens
    inner = jnp.arange(tokens, dtype=jnp.int32)
    positions = (own_at[:, None] + inner[None, :]).reshape(-1)
    other_at = (rank ^ jnp.array([m ^ 1 for m in layout], dtype=jnp.int32)) * tokens
    positions_other = (other_at[:, None] + inner[None, :]).reshape(-1)
    is_even = rank % 2 == 0
    q_own, kv_own, q_other, kv_other = (proj[:, i * head : (i + 1) * head] for i in range(4))
    keys = rotary(jnp.where(is_even, kv_own, kv_other), positions)
    values = jnp.where(is_even, kv_other, kv_own)
    keyval = jnp.concatenate([keys, values], axis=1).astype(jnp.bfloat16)
    keyval = jnp.concatenate([keyval, swap(keyval, "dp", 1)], axis=0)
    queries = jnp.concatenate(
        [rotary(q_own, positions), rotary(q_other, positions)], axis=0
    ).astype(jnp.bfloat16)

    key_at = jnp.concatenate([positions, positions_other])
    query_at = jnp.concatenate([positions, positions])
    scores = lax.dot_general(
        queries, keyval[:, :head], (((1,), (1,)), ((), ())), preferred_element_type=jnp.float32
    ) * ((width / ranks) ** (-0.5))
    capped = 50.0 * jnp.tanh(scores / 50.0)
    expd = jnp.where(key_at[None, :] <= query_at[:, None], jnp.exp(capped), 0.0)
    denominator = jnp.sum(expd, axis=-1, keepdims=True)
    numer = jnp.dot(
        expd.astype(jnp.bfloat16), keyval[:, head:], preferred_element_type=jnp.float32
    )
    attended = (numer / denominator).astype(jnp.bfloat16)
    attended = jnp.concatenate([attended[:half], attended[half:]], axis=1)
    w_out = jnp.concatenate([output_weight[0], wo_other], axis=0)

    sums = []
    for (a, b), order in zip(columns, orders):
        part = jnp.dot(attended, w_out[:, a:b], preferred_element_type=jnp.float32)
        part = part.reshape(-1, tokens, b - a)
        have = span(order)
        if have != layout:
            part = jnp.concatenate([part[layout.index(m)][None] for m in have])
        sums.append(part)
    for stage in reversed(range(len(orders[0]))):
        sent = [
            swap(part[part.shape[0] // 2 :].astype(jnp.bfloat16), "dp", order[stage])
            for part, order in zip(sums, orders)
        ]
        if stage == len(orders[0]) - 1:
            incoming, sums = lax.optimization_barrier((incoming, sums))
            new_accumulators = place_blocks(block_sources, rank, incoming)
        sums = [
            part[: part.shape[0] // 2] + got.astype(jnp.float32) for part, got in zip(sums, sent)
        ]
    summed = jnp.concatenate([part[0] for part in sums], axis=-1)
    check_out = (checked.astype(jnp.float32) + rms_norm(summed, post_gain[0])).astype(jnp.bfloat16)
    return (moved, new_accumulators, check_out[None, :, :])


def solution(mesh):
    placed = (
        P("section", "dp", None),
        P(),
        P("dp", "section", None),
        P(),
        P("section", "dp"),
        P("section", None),
        P("section", None, "dp"),
        P("section", None, "dp"),
        P("section", "dp", None),
        P("section", None),
    )
    return jax.shard_map(
        step,
        mesh=mesh,
        in_specs=placed,
        out_specs=(P("section", "dp", None), P("dp", "section", None), P("section", "dp", None)),
        check_vma=False,
    )
```

profile of v0, /device:TPU:0, one launch (start us, length us, event | category | flops | bytes accessed | tf_op | source)
XLA Modules:
  0.0 80.6 jit_solution(2174184480568152548)
XLA Ops:
  0.7 2.4 %pick_sends.1 = bf16[1,16,4608]{2,1,0:T(8,128)(2,1)} custom-call(s32[4]{0:T(128)} %table.3, s32[1]{0:T(128)} %bitcast.2.own_ref, bf16[2,16,4608]{2,1,0:T(8,128)(2,1)} %held.2), custom_call_target="tpu_custom_call" | custom-call | tf_op jit(solution)/shard_map/pick_sends/pallas_call | solution.py:55
  3.1 3.0 %collective-permute-start = (bf16[16,4608]{1,0:T(8,128)(2,1)}, bf16[16,4608]{1,0:T(8,128)(2,1)S(1)}, u32[]{:S(2)}, u32[]{:S(2)}) collective-permute-start(bf16[16,4608]{1,0:T(8,128)(2,1)} %bitcast.103), channel_id=1, source_target_pairs={{0,16},{16,0},{1,17},{17,1},{2,18},{18,2},{3,19},{19,3},{4,20},{20... | collective-permute-start | bytes 442376 | tf_op jit(solution)/shard_map/ppermute | solution.py:11
  7.3 3.8 %pack_blocks.1 = bf16[16,2,4736]{2,1,0:T(2,128)(2,1)} custom-call(s32[256]{0:T(256)} %table.5, s32[1]{0:T(128)} %bitcast.8.own_ref, f32[16,2,4608]{2,1,0:T(2,128)} %held.3, f32[1,1]{1,0:T(1,128)S(6)} %copy.26.term_ref), custom_call_target="tpu_custom_call" | custom-call | tf_op jit(solution)/shard_map/pack_blocks/pallas_call | solution.py:90
  11.1 6.0 %all-to-all-start = ((bf16[16,2,4736]{2,1,0:T(2,128)(2,1)}), bf16[16,2,4736]{2,1,0:T(2,128)(2,1)S(1)}, u32[]{:S(2)}, u32[]{:S(2)}) async-start(bf16[16,2,4736]{2,1,0:T(2,128)(2,1)} %pack_blocks.1), calls=%async_computation | async-start | bytes 606208 | tf_op jit(solution)/shard_map/all_to_all | solution.py:174
  22.2 3.8 %collective-permute-start.1 = (bf16[1,16,2304]{2,1,0:T(8,128)(2,1)S(1)}, bf16[1,16,2304]{2,1,0:T(8,128)(2,1)S(1)}, u32[]{:S(2)}, u32[]{:S(2)}) collective-permute-start(bf16[1,16,2304]{2,1,0:T(8,128)(2,1)S(1)} %get-tuple-element.27), channel_id=1, source_target_pairs={{0,12},{1,13},{2,14},{3,15},{4,8},{5,9},{6,10},{7,11},{8,4},{9,5},... | collective-permute-start | bytes 221192 | tf_op jit(solution)/shard_map/ppermute | solution.py:11
  26.2 2.6 %collective-permute-done.1 = bf16[1,16,2304]{2,1,0:T(8,128)(2,1)S(1)} collective-permute-done((bf16[1,16,2304]{2,1,0:T(8,128)(2,1)S(1)}, bf16[1,16,2304]{2,1,0:T(8,128)(2,1)S(1)}, u32[]{:S(2)}, u32[]{:S(2)}) %collective-permute-start.1) | collective-permute-done | bytes 73760 | tf_op jit(solution)/shard_map/ppermute | solution.py:11
  28.8 1.7 %collective-permute-start.4 = (bf16[2,16,2304]{2,1,0:T(8,128)(2,1)S(1)}, bf16[2,16,2304]{2,1,0:T(8,128)(2,1)S(1)}, u32[]{:S(2)}, u32[]{:S(2)}) collective-permute-start(bf16[2,16,2304]{2,1,0:T(8,128)(2,1)S(1)} %pad_maximum_fusion.9), channel_id=1, source_target_pairs={{0,2},{1,3},{2,0},{3,1},{4,6},{5,7},{6,4},{7,5},{8,10},{9,11},{10,... | collective-permute-start | bytes 442376 | tf_op jit(solution)/shard_map/ppermute | solution.py:11
  30.4 1.8 %collective-permute-done.5 = bf16[1,16,2304]{2,1,0:T(8,128)(2,1)S(1)} collective-permute-done((bf16[1,16,2304]{2,1,0:T(8,128)(2,1)S(1)}, bf16[1,16,2304]{2,1,0:T(8,128)(2,1)S(1)}, u32[]{:S(2)}, u32[]{:S(2)}) %collective-permute-start.5) | collective-permute-done | bytes 73760 | tf_op jit(solution)/shard_map/ppermute | solution.py:11
  32.3 2.9 %collective-permute-start.6 = (bf16[2,16,2304]{2,1,0:T(8,128)(2,1)S(1)}, bf16[2,16,2304]{2,1,0:T(8,128)(2,1)S(1)}, u32[]{:S(2)}, u32[]{:S(2)}) collective-permute-start(bf16[2,16,2304]{2,1,0:T(8,128)(2,1)S(1)} %pad_maximum_fusion.10), channel_id=1, source_target_pairs={{0,4},{1,5},{2,6},{3,7},{4,0},{5,1},{6,2},{7,3},{8,12},{9,13},{10,... | collective-permute-start | bytes 442376 | tf_op jit(solution)/shard_map/ppermute | solution.py:11
  35.2 1.6 %pad_maximum_fusion = bf16[4608,512]{1,0:T(8,128)(2,1)S(1)} fusion(bf16[4608,128]{1,0:T(8,128)(2,1)} %collective-permute-done.3, bf16[4608,128]{1,0:T(8,128)(2,1)S(1)} %collective-permute-done.2, bf16[4608,128]{1,0:T(8,128)(2,1)S(1)} %bitcast.98, bf16[4608,128]{1,0:T(8,128)(2,1)S(1)} %bitcast.100), kind=kLoop, calls=%fused_computation | loop fusion | flops 18874368 | bytes 9437184 | tf_op jit(solution)/shard_map/concatenate | solution.py:188
  36.8 1.4 %collective-permute-done.6 = bf16[2,16,2304]{2,1,0:T(8,128)(2,1)S(1)} collective-permute-done((bf16[2,16,2304]{2,1,0:T(8,128)(2,1)S(1)}, bf16[2,16,2304]{2,1,0:T(8,128)(2,1)S(1)}, u32[]{:S(2)}, u32[]{:S(2)}) %collective-permute-start.6) | collective-permute-done | bytes 147488 | tf_op jit(solution)/shard_map/ppermute | solution.py:11
  38.3 1.4 %collective-permute-start.8 = (bf16[4,16,2304]{2,1,0:T(8,128)(2,1)S(1)}, bf16[4,16,2304]{2,1,0:T(8,128)(2,1)S(1)}, u32[]{:S(2)}, u32[]{:S(2)}) collective-permute-start(bf16[4,16,2304]{2,1,0:T(8,128)(2,1)S(1)} %pad_maximum_fusion.6), channel_id=1, source_target_pairs={{0,2},{1,3},{2,0},{3,1},{4,6},{5,7},{6,4},{7,5},{8,10},{9,11},{10,... | collective-permute-start | bytes 884744 | tf_op jit(solution)/shard_map/ppermute | solution.py:11
  39.7 1.8 %collective-permute-start.7 = (bf16[4,16,2304]{2,1,0:T(8,128)(2,1)S(1)}, bf16[4,16,2304]{2,1,0:T(8,128)(2,1)S(1)}, u32[]{:S(2)}, u32[]{:S(2)}) collective-permute-start(bf16[4,16,2304]{2,1,0:T(8,128)(2,1)S(1)} %pad_maximum_fusion.5), channel_id=1, source_target_pairs={{0,4},{1,5},{2,6},{3,7},{4,0},{5,1},{6,2},{7,3},{8,12},{9,13},{10,... | collective-permute-start | bytes 884744 | tf_op jit(solution)/shard_map/ppermute | solution.py:11
  41.5 4.3 %collective-permute-done.8 = bf16[4,16,2304]{2,1,0:T(8,128)(2,1)S(1)} collective-permute-done((bf16[4,16,2304]{2,1,0:T(8,128)(2,1)S(1)}, bf16[4,16,2304]{2,1,0:T(8,128)(2,1)S(1)}, u32[]{:S(2)}, u32[]{:S(2)}) %collective-permute-start.8) | collective-permute-done | bytes 294944 | tf_op jit(solution)/shard_map/ppermute | solution.py:11
  46.4 1.0 %collective-permute-done.7 = bf16[4,16,2304]{2,1,0:T(8,128)(2,1)S(1)} collective-permute-done((bf16[4,16,2304]{2,1,0:T(8,128)(2,1)S(1)}, bf16[4,16,2304]{2,1,0:T(8,128)(2,1)S(1)}, u32[]{:S(2)}, u32[]{:S(2)}) %collective-permute-start.7) | collective-permute-done | bytes 294944 | tf_op jit(solution)/shard_map/ppermute | solution.py:11
  48.5 0.7 pad_maximum_fusion.4
  52.8 0.7 fusion.24
  53.5 0.7 fusion.31
  55.9 0.7 fusion.37
  56.6 1.5 %collective-permute-start.11 = (bf16[4,16,2304]{2,1,0:T(8,128)(2,1)S(1)}, bf16[4,16,2304]{2,1,0:T(8,128)(2,1)S(1)}, u32[]{:S(2)}, u32[]{:S(2)}) collective-permute-start(bf16[4,16,2304]{2,1,0:T(8,128)(2,1)S(1)} %bitcast.102), channel_id=1, source_target_pairs={{0,4},{1,5},{2,6},{3,7},{4,0},{5,1},{6,2},{7,3},{8,12},{9,13},{10,... | collective-permute-start | bytes 884744 | tf_op jit(solution)/shard_map/ppermute | solution.py:11
  58.1 0.8 collective-permute-start.14
  58.9 3.0 %place_blocks.1 = f32[16,2,4608]{2,1,0:T(2,128)} custom-call(s32[256]{0:T(256)} %table.5, s32[1]{0:T(128)} %bitcast.8.own_ref, bf16[16,2,4736]{2,1,0:T(2,128)(2,1)} %copy-done.1), custom_call_target="tpu_custom_call" | custom-call | tf_op jit(solution)/shard_map/place_blocks/pallas_call | solution.py:124
  61.9 3.7 %collective-permute-done.11 = bf16[4,16,2304]{2,1,0:T(8,128)(2,1)S(1)} collective-permute-done((bf16[4,16,2304]{2,1,0:T(8,128)(2,1)S(1)}, bf16[4,16,2304]{2,1,0:T(8,128)(2,1)S(1)}, u32[]{:S(2)}, u32[]{:S(2)}) %collective-permute-start.11) | collective-permute-done | bytes 294944 | tf_op jit(solution)/shard_map/ppermute | solution.py:11
  65.7 0.8 collective-permute-start.12
  66.9 1.1 %convert_add_fusion = f32[4,16,2304]{2,1,0:T(8,128)S(1)} fusion(bf16[4,16,2304]{2,1,0:T(8,128)(2,1)S(1)} %collective-permute-done.14, f32[8,16,2304]{2,1,0:T(8,128)} %fusion.37), kind=kLoop, calls=%fused_computation.22 | loop fusion | flops 294912 | bytes 1474560 | tf_op jit(solution)/shard_map/add | solution.py:265
  68.1 1.1 %collective-permute-start.15 = (bf16[2,16,2304]{2,1,0:T(8,128)(2,1)S(1)}, bf16[2,16,2304]{2,1,0:T(8,128)(2,1)S(1)}, u32[]{:S(2)}, u32[]{:S(2)}) collective-permute-start(bf16[2,16,2304]{2,1,0:T(8,128)(2,1)S(1)} %slice.340), channel_id=1, source_target_pairs={{0,4},{1,5},{2,6},{3,7},{4,0},{5,1},{6,2},{7,3},{8,12},{9,13},{10,... | collective-permute-start | bytes 442376 | tf_op jit(solution)/shard_map/ppermute | solution.py:11
  69.2 1.7 %collective-permute-done.12 = bf16[2,16,2304]{2,1,0:T(8,128)(2,1)S(1)} collective-permute-done((bf16[2,16,2304]{2,1,0:T(8,128)(2,1)S(1)}, bf16[2,16,2304]{2,1,0:T(8,128)(2,1)S(1)}, u32[]{:S(2)}, u32[]{:S(2)}) %collective-permute-start.12) | collective-permute-done | bytes 147488 | tf_op jit(solution)/shard_map/ppermute | solution.py:11
  71.0 1.8 %collective-permute-start.13 = (bf16[1,16,2304]{2,1,0:T(8,128)(2,1)S(1)}, bf16[1,16,2304]{2,1,0:T(8,128)(2,1)S(1)}, u32[]{:S(2)}, u32[]{:S(2)}) collective-permute-start(bf16[1,16,2304]{2,1,0:T(8,128)(2,1)S(1)} %slice.343), channel_id=1, source_target_pairs={{0,12},{1,13},{2,14},{3,15},{4,8},{5,9},{6,10},{7,11},{8,4},{9,5},... | collective-permute-start | bytes 221192 | tf_op jit(solution)/shard_map/ppermute | solution.py:11
  73.4 1.7 %collective-permute-start.16 = (bf16[1,16,2304]{2,1,0:T(8,128)(2,1)S(1)}, bf16[1,16,2304]{2,1,0:T(8,128)(2,1)S(1)}, u32[]{:S(2)}, u32[]{:S(2)}) collective-permute-start(bf16[1,16,2304]{2,1,0:T(8,128)(2,1)S(1)} %slice.342), channel_id=1, source_target_pairs={{0,12},{1,13},{2,14},{3,15},{4,8},{5,9},{6,10},{7,11},{8,4},{9,5},... | collective-permute-start | bytes 221192 | tf_op jit(solution)/shard_map/ppermute | solution.py:11
  75.1 2.3 %collective-permute-done.13 = bf16[1,16,2304]{2,1,0:T(8,128)(2,1)S(1)} collective-permute-done((bf16[1,16,2304]{2,1,0:T(8,128)(2,1)S(1)}, bf16[1,16,2304]{2,1,0:T(8,128)(2,1)S(1)}, u32[]{:S(2)}, u32[]{:S(2)}) %collective-permute-start.13) | collective-permute-done | bytes 73760 | tf_op jit(solution)/shard_map/ppermute | solution.py:11
  77.4 2.3 %collective-permute-done.16 = bf16[1,16,2304]{2,1,0:T(8,128)(2,1)S(1)} collective-permute-done((bf16[1,16,2304]{2,1,0:T(8,128)(2,1)S(1)}, bf16[1,16,2304]{2,1,0:T(8,128)(2,1)S(1)}, u32[]{:S(2)}, u32[]{:S(2)}) %collective-permute-start.16) | collective-permute-done | bytes 73760 | tf_op jit(solution)/shard_map/ppermute | solution.py:11
  79.8 0.8 fusion.21
  (93 shorter events, 11.1 us)
Async XLA Ops:
  0.6 17.9 %copy-start.8 = (s32[8]{0:T(128)S(1)}, s32[8]{0:T(128)}, u32[]{:S(2)}) copy-start(s32[8]{0:T(128)} %constant.74.clone) | copy-start | bytes 100
  0.6 17.8 %copy-start.9 = (s32[8]{0:T(128)S(1)}, s32[8]{0:T(128)}, u32[]{:S(2)}) copy-start(s32[8]{0:T(128)} %constant.75.clone) | copy-start | bytes 100
  0.7 16.5 %copy-start.7 = (s32[4]{0:T(128)S(1)}, s32[4]{0:T(128)}, u32[]{:S(2)}) copy-start(s32[4]{0:T(128)} %table.3) | copy-start | bytes 52
  0.7 21.2 %copy-start.4 = (bf16[2,16,4608]{2,1,0:T(8,128)(2,1)S(1)}, bf16[2,16,4608]{2,1,0:T(8,128)(2,1)}, u32[]{:S(2)}) copy-start(bf16[2,16,4608]{2,1,0:T(8,128)(2,1)} %held.2) | copy-start | bytes 884740
  0.7 19.3 %copy-start.5 = (f32[1,4608]{1,0:T(1,128)S(1)}, f32[1,4608]{1,0:T(1,128)}, u32[]{:S(2)}) copy-start(f32[1,4608]{1,0:T(1,128)} %param.17) | copy-start | bytes 55300
  0.7 19.3 %copy-start.6 = (f32[1,4608]{1,0:T(1,128)S(1)}, f32[1,4608]{1,0:T(1,128)}, u32[]{:S(2)}) copy-start(f32[1,4608]{1,0:T(1,128)} %param.21) | copy-start | bytes 55300
  3.1 18.7 %collective-permute-start = (bf16[16,4608]{1,0:T(8,128)(2,1)}, bf16[16,4608]{1,0:T(8,128)(2,1)S(1)}, u32[]{:S(2)}, u32[]{:S(2)}) collective-permute-start(bf16[16,4608]{1,0:T(8,128)(2,1)} %bitcast.103), channel_id=1, source_target_pairs={{0,16},{16,0},{1,17},{17,1},{2,18},{18,2},{3,19},{19,3},{4,20},{20... | collective-permute-start | bytes 442376 | tf_op jit(solution)/shard_map/ppermute | solution.py:11
  6.1 29.0 %collective-permute-start.2 = (bf16[4608,128]{1,0:T(8,128)(2,1)}, bf16[4608,128]{1,0:T(8,128)(2,1)S(1)}, u32[]{:S(2)}, u32[]{:S(2)}) collective-permute-start(bf16[4608,128]{1,0:T(8,128)(2,1)} %bitcast.99), channel_id=1, source_target_pairs={{0,1},{1,0},{2,3},{3,2},{4,5},{5,4},{6,7},{7,6},{8,9},{9,8},{10,11... | collective-permute-start | bytes 3538952 | tf_op jit(solution)/shard_map/ppermute | solution.py:11
  6.1 29.0 %collective-permute-start.3 = (bf16[4608,128]{1,0:T(8,128)(2,1)}, bf16[4608,128]{1,0:T(8,128)(2,1)}, u32[]{:S(2)}, u32[]{:S(2)}) collective-permute-start(bf16[4608,128]{1,0:T(8,128)(2,1)} %bitcast.97), channel_id=1, source_target_pairs={{0,1},{1,0},{2,3},{3,2},{4,5},{5,4},{6,7},{7,6},{8,9},{9,8},{10,11... | collective-permute-start | bytes 3538952 | tf_op jit(solution)/shard_map/ppermute | solution.py:11
  6.6 43.8 %collective-permute-start.10 = (bf16[128,4608]{1,0:T(8,128)(2,1)}, bf16[128,4608]{1,0:T(8,128)(2,1)S(1)}, u32[]{:S(2)}, u32[]{:S(2)}) collective-permute-start(bf16[128,4608]{1,0:T(8,128)(2,1)} %bitcast.92), channel_id=1, source_target_pairs={{0,1},{1,0},{2,3},{3,2},{4,5},{5,4},{6,7},{7,6},{8,9},{9,8},{10,11... | collective-permute-start | bytes 3538952 | tf_op jit(solution)/shard_map/ppermute | solution.py:11
  11.1 45.5 %all-to-all-start = ((bf16[16,2,4736]{2,1,0:T(2,128)(2,1)}), bf16[16,2,4736]{2,1,0:T(2,128)(2,1)S(1)}, u32[]{:S(2)}, u32[]{:S(2)}) async-start(bf16[16,2,4736]{2,1,0:T(2,128)(2,1)} %pack_blocks.1), calls=%async_computation | async-start | bytes 606208 | tf_op jit(solution)/shard_map/all_to_all | solution.py:174
  21.8 13.3 %copy-start.2 = (bf16[1,4608,128]{2,1,0:T(8,128)(2,1)S(1)}, bf16[1,4608,128]{2,1,0:T(8,128)(2,1)}, u32[]{:S(2)}) copy-start(bf16[1,4608,128]{2,1,0:T(8,128)(2,1)} %param.19) | copy-start | bytes 3538948
  21.8 13.3 %copy-start.3 = (bf16[1,4608,128]{2,1,0:T(8,128)(2,1)S(1)}, bf16[1,4608,128]{2,1,0:T(8,128)(2,1)}, u32[]{:S(2)}) copy-start(bf16[1,4608,128]{2,1,0:T(8,128)(2,1)} %param.18) | copy-start | bytes 3538948
  22.2 6.5 %collective-permute-start.1 = (bf16[1,16,2304]{2,1,0:T(8,128)(2,1)S(1)}, bf16[1,16,2304]{2,1,0:T(8,128)(2,1)S(1)}, u32[]{:S(2)}, u32[]{:S(2)}) collective-permute-start(bf16[1,16,2304]{2,1,0:T(8,128)(2,1)S(1)} %get-tuple-element.27), channel_id=1, source_target_pairs={{0,12},{1,13},{2,14},{3,15},{4,8},{5,9},{6,10},{7,11},{8,4},{9,5},... | collective-permute-start | bytes 221192 | tf_op jit(solution)/shard_map/ppermute | solution.py:11
  26.0 6.2 %collective-permute-start.5 = (bf16[1,16,2304]{2,1,0:T(8,128)(2,1)S(1)}, bf16[1,16,2304]{2,1,0:T(8,128)(2,1)S(1)}, u32[]{:S(2)}, u32[]{:S(2)}) collective-permute-start(bf16[1,16,2304]{2,1,0:T(8,128)(2,1)S(1)} %get-tuple-element.28), channel_id=1, source_target_pairs={{0,12},{1,13},{2,14},{3,15},{4,8},{5,9},{6,10},{7,11},{8,4},{9,5},... | collective-permute-start | bytes 221192 | tf_op jit(solution)/shard_map/ppermute | solution.py:11
  28.8 8.1 %collective-permute-start.4 = (bf16[2,16,2304]{2,1,0:T(8,128)(2,1)S(1)}, bf16[2,16,2304]{2,1,0:T(8,128)(2,1)S(1)}, u32[]{:S(2)}, u32[]{:S(2)}) collective-permute-start(bf16[2,16,2304]{2,1,0:T(8,128)(2,1)S(1)} %pad_maximum_fusion.9), channel_id=1, source_target_pairs={{0,2},{1,3},{2,0},{3,1},{4,6},{5,7},{6,4},{7,5},{8,10},{9,11},{10,... | collective-permute-start | bytes 442376 | tf_op jit(solution)/shard_map/ppermute | solution.py:11
  32.3 6.0 %collective-permute-start.6 = (bf16[2,16,2304]{2,1,0:T(8,128)(2,1)S(1)}, bf16[2,16,2304]{2,1,0:T(8,128)(2,1)S(1)}, u32[]{:S(2)}, u32[]{:S(2)}) collective-permute-start(bf16[2,16,2304]{2,1,0:T(8,128)(2,1)S(1)} %pad_maximum_fusion.10), channel_id=1, source_target_pairs={{0,4},{1,5},{2,6},{3,7},{4,0},{5,1},{6,2},{7,3},{8,12},{9,13},{10,... | collective-permute-start | bytes 442376 | tf_op jit(solution)/shard_map/ppermute | solution.py:11
  38.3 7.6 %collective-permute-start.8 = (bf16[4,16,2304]{2,1,0:T(8,128)(2,1)S(1)}, bf16[4,16,2304]{2,1,0:T(8,128)(2,1)S(1)}, u32[]{:S(2)}, u32[]{:S(2)}) collective-permute-start(bf16[4,16,2304]{2,1,0:T(8,128)(2,1)S(1)} %pad_maximum_fusion.6), channel_id=1, source_target_pairs={{0,2},{1,3},{2,0},{3,1},{4,6},{5,7},{6,4},{7,5},{8,10},{9,11},{10,... | collective-permute-start | bytes 884744 | tf_op jit(solution)/shard_map/ppermute | solution.py:11
  39.7 7.7 %collective-permute-start.7 = (bf16[4,16,2304]{2,1,0:T(8,128)(2,1)S(1)}, bf16[4,16,2304]{2,1,0:T(8,128)(2,1)S(1)}, u32[]{:S(2)}, u32[]{:S(2)}) collective-permute-start(bf16[4,16,2304]{2,1,0:T(8,128)(2,1)S(1)} %pad_maximum_fusion.5), channel_id=1, source_target_pairs={{0,4},{1,5},{2,6},{3,7},{4,0},{5,1},{6,2},{7,3},{8,12},{9,13},{10,... | collective-permute-start | bytes 884744 | tf_op jit(solution)/shard_map/ppermute | solution.py:11
  48.5 1.3 %collective-permute-start.9 = (bf16[128,256]{1,0:T(8,128)(2,1)S(1)}, bf16[128,256]{1,0:T(8,128)(2,1)S(1)}, u32[]{:S(2)}, u32[]{:S(2)}) collective-permute-start(bf16[128,256]{1,0:T(8,128)(2,1)S(1)} %pad_maximum_fusion.12), channel_id=1, source_target_pairs={{0,1},{1,0},{2,3},{3,2},{4,5},{5,4},{6,7},{7,6},{8,9},{9,8},{10,11... | collective-permute-start | bytes 196616 | tf_op jit(solution)/shard_map/ppermute | solution.py:11
  48.5 1.9 %copy-start = (bf16[1,128,4608]{2,1,0:T(8,128)(2,1)S(1)}, bf16[1,128,4608]{2,1,0:T(8,128)(2,1)}, u32[]{:S(2)}) copy-start(bf16[1,128,4608]{2,1,0:T(8,128)(2,1)} %param.20) | copy-start | bytes 3538948
  56.6 2.3 %copy-start.1 = (bf16[16,2,4736]{2,1,0:T(2,128)(2,1)}, bf16[16,2,4736]{2,1,0:T(2,128)(2,1)S(1)}, u32[]{:S(2)}) copy-start(bf16[16,2,4736]{2,1,0:T(2,128)(2,1)S(1)} %all-to-all-done.held) | copy-start | bytes 909316
  56.6 9.1 %collective-permute-start.11 = (bf16[4,16,2304]{2,1,0:T(8,128)(2,1)S(1)}, bf16[4,16,2304]{2,1,0:T(8,128)(2,1)S(1)}, u32[]{:S(2)}, u32[]{:S(2)}) collective-permute-start(bf16[4,16,2304]{2,1,0:T(8,128)(2,1)S(1)} %bitcast.102), channel_id=1, source_target_pairs={{0,4},{1,5},{2,6},{3,7},{4,0},{5,1},{6,2},{7,3},{8,12},{9,13},{10,... | collective-permute-start | bytes 884744 | tf_op jit(solution)/shard_map/ppermute | solution.py:11
  58.1 8.9 %collective-permute-start.14 = (bf16[4,16,2304]{2,1,0:T(8,128)(2,1)S(1)}, bf16[4,16,2304]{2,1,0:T(8,128)(2,1)S(1)}, u32[]{:S(2)}, u32[]{:S(2)}) collective-permute-start(bf16[4,16,2304]{2,1,0:T(8,128)(2,1)S(1)} %pad_maximum_fusion.7), channel_id=1, source_target_pairs={{0,2},{1,3},{2,0},{3,1},{4,6},{5,7},{6,4},{7,5},{8,10},{9,11},{10,... | collective-permute-start | bytes 884744 | tf_op jit(solution)/shard_map/ppermute | solution.py:11
  65.7 5.2 %collective-permute-start.12 = (bf16[2,16,2304]{2,1,0:T(8,128)(2,1)S(1)}, bf16[2,16,2304]{2,1,0:T(8,128)(2,1)S(1)}, u32[]{:S(2)}, u32[]{:S(2)}) collective-permute-start(bf16[2,16,2304]{2,1,0:T(8,128)(2,1)S(1)} %slice.341), channel_id=1, source_target_pairs={{0,2},{1,3},{2,0},{3,1},{4,6},{5,7},{6,4},{7,5},{8,10},{9,11},{10,... | collective-permute-start | bytes 442376 | tf_op jit(solution)/shard_map/ppermute | solution.py:11
  68.1 5.2 %collective-permute-start.15 = (bf16[2,16,2304]{2,1,0:T(8,128)(2,1)S(1)}, bf16[2,16,2304]{2,1,0:T(8,128)(2,1)S(1)}, u32[]{:S(2)}, u32[]{:S(2)}) collective-permute-start(bf16[2,16,2304]{2,1,0:T(8,128)(2,1)S(1)} %slice.340), channel_id=1, source_target_pairs={{0,4},{1,5},{2,6},{3,7},{4,0},{5,1},{6,2},{7,3},{8,12},{9,13},{10,... | collective-permute-start | bytes 442376 | tf_op jit(solution)/shard_map/ppermute | solution.py:11
  71.0 6.4 %collective-permute-start.13 = (bf16[1,16,2304]{2,1,0:T(8,128)(2,1)S(1)}, bf16[1,16,2304]{2,1,0:T(8,128)(2,1)S(1)}, u32[]{:S(2)}, u32[]{:S(2)}) collective-permute-start(bf16[1,16,2304]{2,1,0:T(8,128)(2,1)S(1)} %slice.343), channel_id=1, source_target_pairs={{0,12},{1,13},{2,14},{3,15},{4,8},{5,9},{6,10},{7,11},{8,4},{9,5},... | collective-permute-start | bytes 221192 | tf_op jit(solution)/shard_map/ppermute | solution.py:11
  73.4 6.3 %collective-permute-start.16 = (bf16[1,16,2304]{2,1,0:T(8,128)(2,1)S(1)}, bf16[1,16,2304]{2,1,0:T(8,128)(2,1)S(1)}, u32[]{:S(2)}, u32[]{:S(2)}) collective-permute-start(bf16[1,16,2304]{2,1,0:T(8,128)(2,1)S(1)} %slice.342), channel_id=1, source_target_pairs={{0,12},{1,13},{2,14},{3,15},{4,8},{5,9},{6,10},{7,11},{8,4},{9,5},... | collective-permute-start | bytes 221192 | tf_op jit(solution)/shard_map/ppermute | solution.py:11
where the time goes:
time: 81 us; the launch traced here: 80.6 us
  starting transfers between devices  29 us (36%)
  waiting for transfers between devices  22.6 us (28%)
  Pallas kernels  9.21 us (11%)
  other arithmetic  6.58 us (8%)
  local copies, waits for them, and re-layouts  6.44 us (8%)
  between operations  4.59 us (6%)
  matrix products  2.19 us (3%)
    ppermute x17, starting transfers between devices, swap(): return lax.ppermute(value, axis, pairs)  23 us
    ppermute x17, waiting for transfers between devices, swap(): return lax.ppermute(value, axis, pairs)  22.6 us
    all_to_all x1, starting transfers between devices, step(): lax.all_to_all(outgoing, 'dp', split_axis=0, concat_axis=0, tiled=True)  6.05 us
    unnamed x31, local copies, waits for them, and re-layouts  4.76 us
    pallas_call x1, Pallas kernels, pack_blocks(): pl.pallas_call(body, out_shape=jax.ShapeDtypeStruct((groups, rows, width...  3.78 us
    pallas_call x1, Pallas kernels, place_blocks(): pl.pallas_call(body, out_shape=jax.ShapeDtypeStruct((groups, rows, width)...  3.05 us
    pallas_call x1, Pallas kernels, pick_sends(): pl.pallas_call(body, out_shape=jax.ShapeDtypeStruct((groups - 1,) + items...  2.39 us
    concatenate x1, other arithmetic, step(): jnp.concatenate([query_weight[0], keyval_weight[0], wq_other, wkv_other],...  1.64 us
  transfers between devices with their start and end apart: 18, of which 12 were waited for; matrix products, arithmetic and copies ran while one was open for 18% of the time, Pallas kernels for 8%

commit v1 on v0

--- a/solution.py
+++ b/solution.py
@@ -32,9 +32,11 @@
 
 
 def place_for(table, peer, own, groups):
+    shift = groups.bit_length() - 1
+
     def look(j, place):
         entry = table[peer * groups + j]
-        return place + jnp.where(entry // groups == own, entry % groups, 0)
+        return place + jnp.where(entry >> shift == own, entry & (groups - 1), 0)
 
     return lax.fori_loop(0, groups, look, jnp.int32(0), unroll=True)
 
@@ -60,8 +62,9 @@
             pl.BlockSpec(memory_space=pltpu.SMEM),
             pl.BlockSpec(memory_space=pl.ANY),
         ],
-        out_specs=pl.BlockSpec(memory_space=pltpu.VMEM),
+        out_specs=pl.BlockSpec(memory_space=pl.ANY),
         scratch_shapes=[pltpu.SemaphoreType.DMA((groups - 1,))],
+        compiler_params=pltpu.CompilerParams(vmem_limit_bytes=2**20),
         name="pick_sends",
     )(sources, section[None], items)
 
@@ -97,6 +100,7 @@
             pl.BlockSpec(memory_space=pltpu.SMEM),
         ],
         out_specs=pl.BlockSpec(memory_space=pltpu.VMEM),
+        compiler_params=pltpu.CompilerParams(vmem_limit_bytes=2**20 + 4 * blocks.nbytes),
         name="pack_blocks",
     )(sources, rank[None], blocks, term)
 
@@ -115,7 +119,7 @@
         factor = groups / jnp.sum(total, axis=0, keepdims=True)[:, :1]
 
         def one(slot, carry):
-            owner = table[own * groups + slot] // groups
+            owner = table[own * groups + slot] >> (groups.bit_length() - 1)
             out[slot] = held[owner, :, :width].astype(jnp.float32) * factor
             return carry
 
@@ -130,6 +134,7 @@
             pl.BlockSpec(memory_space=pltpu.VMEM),
         ],
         out_specs=pl.BlockSpec(memory_space=pltpu.VMEM),
+        compiler_params=pltpu.CompilerParams(vmem_limit_bytes=2**20 + 8 * blocks.nbytes),
         name="place_blocks",
     )(sources, rank[None], blocks)
 
@@ -139,6 +144,12 @@
     for mask in masks:
         order = order + [entry ^ mask for entry in order]
     return order
+
+
+def turn(values, axes):
+    bits = values.reshape((2,) * axes + (-1, values.shape[-1]))
+    order = tuple(reversed(range(axes))) + (axes, axes + 1)
+    return bits.transpose(order).reshape(values.shape)
 
 
 def step(
@@ -203,18 +214,14 @@
         if stage == 1:
             weights, sent = lax.optimization_barrier((weights, sent))
         parts = [jnp.concatenate([part, got]) for part, got in zip(parts, sent)]
-    rows = []
-    for part, order in zip(parts, orders):
-        have = span(order)
-        if have != layout:
-            part = jnp.concatenate([part[have.index(m)][None] for m in layout])
-        rows.append(part.reshape(-1, part.shape[-1]))
+    rows = [part.reshape(-1, part.shape[-1]) for part in parts]
     half = rows[0].shape[0]
 
-    proj = sum(
+    proj = [
         jnp.dot(part, weights[a:b], preferred_element_type=jnp.float32)
         for part, (a, b) in zip(rows, columns)
-    )
+    ]
+    proj = proj[0] + turn(proj[1], len(rest))
     own_at = (rank ^ jnp.array(layout, dtype=jnp.int32)) * tokens
     inner = jnp.arange(tokens, dtype=jnp.int32)
     positions = (own_at[:, None] + inner[None, :]).reshape(-1)
@@ -246,24 +253,18 @@
     w_out = jnp.concatenate([output_weight[0], wo_other], axis=0)
 
     sums = []
-    for (a, b), order in zip(columns, orders):
-        part = jnp.dot(attended, w_out[:, a:b], preferred_element_type=jnp.float32)
-        part = part.reshape(-1, tokens, b - a)
-        have = span(order)
-        if have != layout:
-            part = jnp.concatenate([part[layout.index(m)][None] for m in have])
-        sums.append(part)
+    for (a, b), source in zip(columns, [attended, turn(attended, len(rest))]):
+        part = jnp.dot(source, w_out[:, a:b], preferred_element_type=jnp.float32)
+        sums.append(part.reshape(-1, tokens, b - a))
     for stage in reversed(range(len(orders[0]))):
         sent = [
             swap(part[part.shape[0] // 2 :].astype(jnp.bfloat16), "dp", order[stage])
             for part, order in zip(sums, orders)
         ]
-        if stage == len(orders[0]) - 1:
-            incoming, sums = lax.optimization_barrier((incoming, sums))
-            new_accumulators = place_blocks(block_sources, rank, incoming)
         sums = [
             part[: part.shape[0] // 2] + got.astype(jnp.float32) for part, got in zip(sums, sent)
         ]
+    new_accumulators = place_blocks(block_sources, rank, incoming)
     summed = jnp.concatenate([part[0] for part in sums], axis=-1)
     check_out = (checked.astype(jnp.float32) + rms_norm(summed, post_gain[0])).astype(jnp.bfloat16)
     return (moved, new_accumulators, check_out[None, :, :])

time: 81 us -> 81.8 us (level)
  Pallas kernels: 9.21 us -> 5.44 us
  other arithmetic: 6.58 us -> 9.22 us
  local copies, waits for them, and re-layouts: 6.44 us -> 8.74 us
  starting transfers between devices: 29 us -> 27.6 us
    pallas_call x1, Pallas kernels: 3.78 us -> 2.07 us  [pack_blocks(): pl.pallas_call(body, out_shape=jax.ShapeDtypeStruct((groups, rows, width...]
    pallas_call x1, Pallas kernels: 2.39 us -> 0.75 us  [pick_sends(): pl.pallas_call(body, out_shape=jax.ShapeDtypeStruct((groups - 1,) + items...]
    ppermute x17, starting transfers between devices: 23 us -> 21.6 us  [swap(): return lax.ppermute(value, axis, pairs)]
    another operation x2, other arithmetic: 0.76 us -> 1.67 us  [step(): moved = jnp.stack([checked] + [slot(j) for j in range(1, sections)])]
    concatenate x2 -> x1, local copies, waits for them, and re-layouts: 0.69 us -> 1.58 us  [step(): attended = jnp.concatenate([attended[:half], attended[half:]], axis=1)]
    transpose x0 -> x2, local copies, waits for them, and re-layouts: none -> 0.86 us  [turn(): return bits.transpose(order).reshape(values.shape)]
    unnamed x31 -> x36, local copies, waits for them, and re-layouts: 4.76 us -> 4.46 us
  transfers between devices with their start and end apart: 18 -> 18, of which waited for: 12 -> 11; matrix products, arithmetic and copies ran while one was open for 18% -> 17% of each run, Pallas kernels for 8% -> 6%
where the time goes in v1:
time: 81.8 us; the launch traced here: 81.2 us
  starting transfers between devices  27.6 us (34%)
  waiting for transfers between devices  23.1 us (28%)
  other arithmetic  9.22 us (11%)
  local copies, waits for them, and re-layouts  8.74 us (11%)
  Pallas kernels  5.44 us (7%)
  between operations  4.99 us (6%)
  matrix products  2.16 us (3%)
    ppermute x17, waiting for transfers between devices, swap(): return lax.ppermute(value, axis, pairs)  23.1 us
    ppermute x17, starting transfers between devices, swap(): return lax.ppermute(value, axis, pairs)  21.6 us
    all_to_all x1, starting transfers between devices, step(): lax.all_to_all(outgoing, 'dp', split_axis=0, concat_axis=0, tiled=True)  6.05 us
    unnamed x36, local copies, waits for them, and re-layouts  4.46 us
    pallas_call x1, Pallas kernels, place_blocks(): pl.pallas_call(body, out_shape=jax.ShapeDtypeStruct((groups, rows, width)...  2.62 us
    concatenate x1, other arithmetic, step(): jnp.concatenate([query_weight[0], keyval_weight[0], wq_other, wkv_other],...  2.24 us
    pallas_call x1, Pallas kernels, pack_blocks(): pl.pallas_call(body, out_shape=jax.ShapeDtypeStruct((groups, rows, width...  2.07 us
    another operation x2, other arithmetic, step(): moved = jnp.stack([checked] + [slot(j) for j in range(1, sections)])  1.67 us
  transfers between devices with their start and end apart: 18, of which 11 were waited for; matrix products, arithmetic and copies ran while one was open for 17% of the time, Pallas kernels for 6%

profile of v1, /device:TPU:0, one launch (start us, length us, event | category | flops | bytes accessed | tf_op | source)
XLA Modules:
  0.0 81.2 jit_solution(17369997368076053085)
XLA Ops:
  0.7 1.0 %copy-done = bf16[2,16,4608]{2,1,0:T(8,128)(2,1)S(1)} copy-done((bf16[2,16,4608]{2,1,0:T(8,128)(2,1)S(1)}, bf16[2,16,4608]{2,1,0:T(8,128)(2,1)}, u32[]{:S(2)}) %copy-start) | copy-done | bytes 294936
  3.1 3.0 %collective-permute-start = (bf16[16,4608]{1,0:T(8,128)(2,1)S(1)}, bf16[16,4608]{1,0:T(8,128)(2,1)S(1)}, u32[]{:S(2)}, u32[]{:S(2)}) collective-permute-start(bf16[16,4608]{1,0:T(8,128)(2,1)S(1)} %bitcast.67), channel_id=1, source_target_pairs={{0,16},{16,0},{1,17},{17,1},{2,18},{18,2},{3,19},{19,3},{4,20},{20... | collective-permute-start | bytes 442376 | tf_op jit(solution)/shard_map/ppermute | solution.py:11
  7.3 1.1 %copy-done.2 = f32[16,2,4608]{2,1,0:T(2,128)S(1)} copy-done((f32[16,2,4608]{2,1,0:T(2,128)S(1)}, f32[16,2,4608]{2,1,0:T(2,128)}, u32[]{:S(2)}) %copy-start.2) | copy-done | bytes 589848
  9.0 2.1 %pack_blocks.1 = bf16[16,2,4736]{2,1,0:T(2,128)(2,1)} custom-call(s32[256]{0:T(256)S(1)} %copy-done.3, s32[1]{0:T(128)} %bitcast.8.own_ref, f32[16,2,4608]{2,1,0:T(2,128)S(1)} %copy-done.2, f32[1,1]{1,0:T(1,128)S(6)} %copy.20.term_ref), custom_call_target="tpu_custom_call" | custom-call | tf_op jit(solution)/shard_map/pack_blocks/pallas_call | solution.py:93
  11.1 6.0 %all-to-all-start = ((bf16[16,2,4736]{2,1,0:T(2,128)(2,1)}), bf16[16,2,4736]{2,1,0:T(2,128)(2,1)S(1)}, u32[]{:S(2)}, u32[]{:S(2)}) async-start(bf16[16,2,4736]{2,1,0:T(2,128)(2,1)} %pack_blocks.1), calls=%async_computation | async-start | bytes 606208 | tf_op jit(solution)/shard_map/all_to_all | solution.py:185
  23.7 3.8 %collective-permute-start.1 = (bf16[1,16,2304]{2,1,0:T(8,128)(2,1)S(1)}, bf16[1,16,2304]{2,1,0:T(8,128)(2,1)S(1)}, u32[]{:S(2)}, u32[]{:S(2)}) collective-permute-start(bf16[1,16,2304]{2,1,0:T(8,128)(2,1)S(1)} %get-tuple-element.18), channel_id=1, source_target_pairs={{0,12},{1,13},{2,14},{3,15},{4,8},{5,9},{6,10},{7,11},{8,4},{9,5},... | collective-permute-start | bytes 221192 | tf_op jit(solution)/shard_map/ppermute | solution.py:11
  27.5 0.9 %fusion.28 = bf16[1,16,4608]{2,1,0:T(8,128)(2,1)S(1)} fusion(bf16[16,4608]{1,0:T(8,128)(2,1)} %copy-done.12, pred[]{:T(512)S(6)} %eq.22, bf16[2,16,4608]{2,1,0:T(8,128)(2,1)S(1)} %copy-done.1, s32[]{:T(128)S(6)} %select_n.64), kind=kLoop, calls=%fused_computation.55 | loop fusion | flops 73728 | bytes 442373 | tf_op jit(solution)/shard_map/stack | solution.py:194
  28.5 1.7 %collective-permute-done.1 = bf16[1,16,2304]{2,1,0:T(8,128)(2,1)S(1)} collective-permute-done((bf16[1,16,2304]{2,1,0:T(8,128)(2,1)S(1)}, bf16[1,16,2304]{2,1,0:T(8,128)(2,1)S(1)}, u32[]{:S(2)}, u32[]{:S(2)}) %collective-permute-start.1) | collective-permute-done | bytes 73760 | tf_op jit(solution)/shard_map/ppermute | solution.py:11
  30.2 1.7 %collective-permute-start.4 = (bf16[2,16,2304]{2,1,0:T(8,128)(2,1)S(1)}, bf16[2,16,2304]{2,1,0:T(8,128)(2,1)S(1)}, u32[]{:S(2)}, u32[]{:S(2)}) collective-permute-start(bf16[2,16,2304]{2,1,0:T(8,128)(2,1)S(1)} %pad_maximum_fusion.9), channel_id=1, source_target_pairs={{0,2},{1,3},{2,0},{3,1},{4,6},{5,7},{6,4},{7,5},{8,10},{9,11},{10,... | collective-permute-start | bytes 442376 | tf_op jit(solution)/shard_map/ppermute | solution.py:11
  31.9 1.7 %collective-permute-done.5 = bf16[1,16,2304]{2,1,0:T(8,128)(2,1)S(1)} collective-permute-done((bf16[1,16,2304]{2,1,0:T(8,128)(2,1)S(1)}, bf16[1,16,2304]{2,1,0:T(8,128)(2,1)S(1)}, u32[]{:S(2)}, u32[]{:S(2)}) %collective-permute-start.5) | collective-permute-done | bytes 73760 | tf_op jit(solution)/shard_map/ppermute | solution.py:11
  33.6 1.1 %collective-permute-start.6 = (bf16[2,16,2304]{2,1,0:T(8,128)(2,1)S(1)}, bf16[2,16,2304]{2,1,0:T(8,128)(2,1)S(1)}, u32[]{:S(2)}, u32[]{:S(2)}) collective-permute-start(bf16[2,16,2304]{2,1,0:T(8,128)(2,1)S(1)} %pad_maximum_fusion.10), channel_id=1, source_target_pairs={{0,4},{1,5},{2,6},{3,7},{4,0},{5,1},{6,2},{7,3},{8,12},{9,13},{10,... | collective-permute-start | bytes 442376 | tf_op jit(solution)/shard_map/ppermute | solution.py:11
  34.8 2.2 %pad_maximum_fusion = bf16[4608,512]{1,0:T(8,128)(2,1)S(1)} fusion(bf16[4608,128]{1,0:T(8,128)(2,1)} %collective-permute-done.3, bf16[4608,128]{1,0:T(8,128)(2,1)} %collective-permute-done.2, bf16[4608,128]{1,0:T(8,128)(2,1)S(1)} %bitcast.75, bf16[4608,128]{1,0:T(8,128)(2,1)} %bitcast.77), kind=kLoop, calls=%fused_computation | loop fusion | flops 18874368 | bytes 9437184 | tf_op jit(solution)/shard_map/concatenate | solution.py:199
  37.0 1.8 %collective-permute-done.6 = bf16[2,16,2304]{2,1,0:T(8,128)(2,1)S(1)} collective-permute-done((bf16[2,16,2304]{2,1,0:T(8,128)(2,1)S(1)}, bf16[2,16,2304]{2,1,0:T(8,128)(2,1)S(1)}, u32[]{:S(2)}, u32[]{:S(2)}) %collective-permute-start.6) | collective-permute-done | bytes 147488 | tf_op jit(solution)/shard_map/ppermute | solution.py:11
  38.9 1.5 %collective-permute-start.8 = (bf16[4,16,2304]{2,1,0:T(8,128)(2,1)S(1)}, bf16[4,16,2304]{2,1,0:T(8,128)(2,1)S(1)}, u32[]{:S(2)}, u32[]{:S(2)}) collective-permute-start(bf16[4,16,2304]{2,1,0:T(8,128)(2,1)S(1)} %pad_maximum_fusion.7), channel_id=1, source_target_pairs={{0,2},{1,3},{2,0},{3,1},{4,6},{5,7},{6,4},{7,5},{8,10},{9,11},{10,... | collective-permute-start | bytes 884744 | tf_op jit(solution)/shard_map/ppermute | solution.py:11
  40.4 1.2 %collective-permute-start.7 = (bf16[4,16,2304]{2,1,0:T(8,128)(2,1)S(1)}, bf16[4,16,2304]{2,1,0:T(8,128)(2,1)S(1)}, u32[]{:S(2)}, u32[]{:S(2)}) collective-permute-start(bf16[4,16,2304]{2,1,0:T(8,128)(2,1)S(1)} %pad_maximum_fusion.6), channel_id=1, source_target_pairs={{0,4},{1,5},{2,6},{3,7},{4,0},{5,1},{6,2},{7,3},{8,12},{9,13},{10,... | collective-permute-start | bytes 884744 | tf_op jit(solution)/shard_map/ppermute | solution.py:11
  41.6 4.0 %collective-permute-done.8 = bf16[4,16,2304]{2,1,0:T(8,128)(2,1)S(1)} collective-permute-done((bf16[4,16,2304]{2,1,0:T(8,128)(2,1)S(1)}, bf16[4,16,2304]{2,1,0:T(8,128)(2,1)S(1)}, u32[]{:S(2)}, u32[]{:S(2)}) %collective-permute-start.8) | collective-permute-done | bytes 294944 | tf_op jit(solution)/shard_map/ppermute | solution.py:11
  46.2 1.0 %collective-permute-done.7 = bf16[4,16,2304]{2,1,0:T(8,128)(2,1)S(1)} collective-permute-done((bf16[4,16,2304]{2,1,0:T(8,128)(2,1)S(1)}, bf16[4,16,2304]{2,1,0:T(8,128)(2,1)S(1)}, u32[]{:S(2)}, u32[]{:S(2)}) %collective-permute-start.7) | collective-permute-done | bytes 294944 | tf_op jit(solution)/shard_map/ppermute | solution.py:11
  49.1 2.6 %place_blocks.1 = f32[16,2,4608]{2,1,0:T(2,128)} custom-call(s32[256]{0:T(256)S(1)} %copy-done.4, s32[1]{0:T(128)} %bitcast.8.own_ref, bf16[16,2,4736]{2,1,0:T(2,128)(2,1)S(1)} %all-to-all-done.held), custom_call_target="tpu_custom_call" | custom-call | tf_op jit(solution)/shard_map/place_blocks/pallas_call | solution.py:128
  53.4 0.8 slice.233
  54.2 1.1 %collective-permute-start.11 = (bf16[4,16,2304]{2,1,0:T(8,128)(2,1)}, bf16[4,16,2304]{2,1,0:T(8,128)(2,1)}, u32[]{:S(2)}, u32[]{:S(2)}) collective-permute-start(bf16[4,16,2304]{2,1,0:T(8,128)(2,1)} %bitcast.21), channel_id=1, source_target_pairs={{0,4},{1,5},{2,6},{3,7},{4,0},{5,1},{6,2},{7,3},{8,12},{9,13},{10,... | collective-permute-start | bytes 884744 | tf_op jit(solution)/shard_map/ppermute | solution.py:11
  55.9 1.6 %copy.17 = bf16[128,256]{1,0:T(8,128)(2,1)} copy(bf16[128,256]{0,1:T(8,128)(2,1)} %pad_maximum_fusion.13) | data formatting | bytes 131072 | tf_op jit(solution)/shard_map/concatenate | solution.py:252
  57.5 0.8 %copy.18 = bf16[2,2,32,256]{3,2,1,0:T(8,128)(2,1)S(1)} copy(bf16[2,2,32,256]{3,2,0,1:T(8,128)(2,1)} %bitcast.83) | data formatting | bytes 131072 | tf_op jit(solution)/shard_map/transpose | solution.py:152
  59.4 4.5 %collective-permute-done.11 = bf16[4,16,2304]{2,1,0:T(8,128)(2,1)} collective-permute-done((bf16[4,16,2304]{2,1,0:T(8,128)(2,1)}, bf16[4,16,2304]{2,1,0:T(8,128)(2,1)}, u32[]{:S(2)}, u32[]{:S(2)}) %collective-permute-start.11) | collective-permute-done | bytes 294944 | tf_op jit(solution)/shard_map/ppermute | solution.py:11
  63.9 1.0 %convert_add_fusion.1 = f32[4,16,2304]{2,1,0:T(8,128)S(1)} fusion(f32[4,16,2304]{2,1,0:T(8,128)S(1)} %bitcast.71, bf16[4,16,2304]{2,1,0:T(8,128)(2,1)} %collective-permute-done.11), kind=kLoop, calls=%fused_computation.27 | loop fusion | flops 294912 | bytes 1474560 | tf_op jit(solution)/shard_map/add | solution.py:265
  65.6 3.1 %collective-permute-done.14 = bf16[4,16,2304]{2,1,0:T(8,128)(2,1)S(1)} collective-permute-done((bf16[4,16,2304]{2,1,0:T(8,128)(2,1)S(1)}, bf16[4,16,2304]{2,1,0:T(8,128)(2,1)S(1)}, u32[]{:S(2)}, u32[]{:S(2)}) %collective-permute-start.14) | collective-permute-done | bytes 294944 | tf_op jit(solution)/shard_map/ppermute | solution.py:11
  68.8 0.8 collective-permute-start.15
  69.5 1.6 %collective-permute-done.12 = bf16[2,16,2304]{2,1,0:T(8,128)(2,1)S(1)} collective-permute-done((bf16[2,16,2304]{2,1,0:T(8,128)(2,1)S(1)}, bf16[2,16,2304]{2,1,0:T(8,128)(2,1)S(1)}, u32[]{:S(2)}, u32[]{:S(2)}) %collective-permute-start.12) | collective-permute-done | bytes 147488 | tf_op jit(solution)/shard_map/ppermute | solution.py:11
  71.2 2.7 %collective-permute-start.13 = (bf16[1,16,2304]{2,1,0:T(8,128)(2,1)S(1)}, bf16[1,16,2304]{2,1,0:T(8,128)(2,1)S(1)}, u32[]{:S(2)}, u32[]{:S(2)}) collective-permute-start(bf16[1,16,2304]{2,1,0:T(8,128)(2,1)S(1)} %slice.237), channel_id=1, source_target_pairs={{0,12},{1,13},{2,14},{3,15},{4,8},{5,9},{6,10},{7,11},{8,4},{9,5},... | collective-permute-start | bytes 221192 | tf_op jit(solution)/shard_map/ppermute | solution.py:11
  74.0 2.7 %collective-permute-start.16 = (bf16[1,16,2304]{2,1,0:T(8,128)(2,1)S(1)}, bf16[1,16,2304]{2,1,0:T(8,128)(2,1)S(1)}, u32[]{:S(2)}, u32[]{:S(2)}) collective-permute-start(bf16[1,16,2304]{2,1,0:T(8,128)(2,1)S(1)} %slice.236), channel_id=1, source_target_pairs={{0,12},{1,13},{2,14},{3,15},{4,8},{5,9},{6,10},{7,11},{8,4},{9,5},... | collective-permute-start | bytes 221192 | tf_op jit(solution)/shard_map/ppermute | solution.py:11
  76.7 0.8 collective-permute-done.13
  77.5 2.7 %collective-permute-done.16 = bf16[1,16,2304]{2,1,0:T(8,128)(2,1)S(1)} collective-permute-done((bf16[1,16,2304]{2,1,0:T(8,128)(2,1)S(1)}, bf16[1,16,2304]{2,1,0:T(8,128)(2,1)S(1)}, u32[]{:S(2)}, u32[]{:S(2)}) %collective-permute-start.16) | collective-permute-done | bytes 73760 | tf_op jit(solution)/shard_map/ppermute | solution.py:11
  80.4 0.8 fusion.25
  (103 shorter events, 12.6 us)
Async XLA Ops:
  0.6 17.9 %copy-start.16 = (s32[8]{0:T(128)S(1)}, s32[8]{0:T(128)}, u32[]{:S(2)}) copy-start(s32[8]{0:T(128)} %constant.74.clone) | copy-start | bytes 100
  0.6 17.9 %copy-start.17 = (s32[8]{0:T(128)S(1)}, s32[8]{0:T(128)}, u32[]{:S(2)}) copy-start(s32[8]{0:T(128)} %constant.75.clone) | copy-start | bytes 100
  0.7 16.5 %copy-start.6 = (s32[4]{0:T(128)S(1)}, s32[4]{0:T(128)}, u32[]{:S(2)}) copy-start(s32[4]{0:T(128)} %table.3) | copy-start | bytes 52
  2.3 17.9 %copy-start.14 = (f32[1,4608]{1,0:T(1,128)S(1)}, f32[1,4608]{1,0:T(1,128)}, u32[]{:S(2)}) copy-start(f32[1,4608]{1,0:T(1,128)} %param.17) | copy-start | bytes 55300
  2.3 17.9 %copy-start.15 = (f32[1,4608]{1,0:T(1,128)S(1)}, f32[1,4608]{1,0:T(1,128)}, u32[]{:S(2)}) copy-start(f32[1,4608]{1,0:T(1,128)} %param.21) | copy-start | bytes 55300
  2.3 20.6 %copy-start.1 = (bf16[2,16,4608]{2,1,0:T(8,128)(2,1)S(1)}, bf16[2,16,4608]{2,1,0:T(8,128)(2,1)}, u32[]{:S(2)}) copy-start(bf16[2,16,4608]{2,1,0:T(8,128)(2,1)} %held.2) | copy-start | bytes 884740
  3.1 19.8 %collective-permute-start = (bf16[16,4608]{1,0:T(8,128)(2,1)S(1)}, bf16[16,4608]{1,0:T(8,128)(2,1)S(1)}, u32[]{:S(2)}, u32[]{:S(2)}) collective-permute-start(bf16[16,4608]{1,0:T(8,128)(2,1)S(1)} %bitcast.67), channel_id=1, source_target_pairs={{0,16},{16,0},{1,17},{17,1},{2,18},{18,2},{3,19},{19,3},{4,20},{20... | collective-permute-start | bytes 442376 | tf_op jit(solution)/shard_map/ppermute | solution.py:11
  6.1 28.7 %collective-permute-start.2 = (bf16[4608,128]{1,0:T(8,128)(2,1)}, bf16[4608,128]{1,0:T(8,128)(2,1)}, u32[]{:S(2)}, u32[]{:S(2)}) collective-permute-start(bf16[4608,128]{1,0:T(8,128)(2,1)} %bitcast.76), channel_id=1, source_target_pairs={{0,1},{1,0},{2,3},{3,2},{4,5},{5,4},{6,7},{7,6},{8,9},{9,8},{10,11... | collective-permute-start | bytes 3538952 | tf_op jit(solution)/shard_map/ppermute | solution.py:11
  6.1 28.7 %collective-permute-start.3 = (bf16[4608,128]{1,0:T(8,128)(2,1)}, bf16[4608,128]{1,0:T(8,128)(2,1)}, u32[]{:S(2)}, u32[]{:S(2)}) collective-permute-start(bf16[4608,128]{1,0:T(8,128)(2,1)} %bitcast.74), channel_id=1, source_target_pairs={{0,1},{1,0},{2,3},{3,2},{4,5},{5,4},{6,7},{7,6},{8,9},{9,8},{10,11... | collective-permute-start | bytes 3538952 | tf_op jit(solution)/shard_map/ppermute | solution.py:11
  6.6 45.8 %collective-permute-start.10 = (bf16[128,4608]{1,0:T(8,128)(2,1)}, bf16[128,4608]{1,0:T(8,128)(2,1)S(1)}, u32[]{:S(2)}, u32[]{:S(2)}) collective-permute-start(bf16[128,4608]{1,0:T(8,128)(2,1)} %bitcast.68), channel_id=1, source_target_pairs={{0,1},{1,0},{2,3},{3,2},{4,5},{5,4},{6,7},{7,6},{8,9},{9,8},{10,11... | collective-permute-start | bytes 3538952 | tf_op jit(solution)/shard_map/ppermute | solution.py:11
  11.1 38.0 %all-to-all-start = ((bf16[16,2,4736]{2,1,0:T(2,128)(2,1)}), bf16[16,2,4736]{2,1,0:T(2,128)(2,1)S(1)}, u32[]{:S(2)}, u32[]{:S(2)}) async-start(bf16[16,2,4736]{2,1,0:T(2,128)(2,1)} %pack_blocks.1), calls=%async_computation | async-start | bytes 606208 | tf_op jit(solution)/shard_map/all_to_all | solution.py:185
  17.1 17.6 %copy-start.11 = (bf16[1,4608,128]{2,1,0:T(8,128)(2,1)S(1)}, bf16[1,4608,128]{2,1,0:T(8,128)(2,1)}, u32[]{:S(2)}) copy-start(bf16[1,4608,128]{2,1,0:T(8,128)(2,1)} %param.19) | copy-start | bytes 3538948
  23.1 25.3 %copy-start.9 = (bf16[16,4608]{1,0:T(8,128)(2,1)}, bf16[16,4608]{1,0:T(8,128)(2,1)S(1)}, u32[]{:S(2)}) copy-start(bf16[16,4608]{1,0:T(8,128)(2,1)S(1)} %get-tuple-element.10) | copy-start | bytes 442372
  23.7 6.5 %collective-permute-start.1 = (bf16[1,16,2304]{2,1,0:T(8,128)(2,1)S(1)}, bf16[1,16,2304]{2,1,0:T(8,128)(2,1)S(1)}, u32[]{:S(2)}, u32[]{:S(2)}) collective-permute-start(bf16[1,16,2304]{2,1,0:T(8,128)(2,1)S(1)} %get-tuple-element.18), channel_id=1, source_target_pairs={{0,12},{1,13},{2,14},{3,15},{4,8},{5,9},{6,10},{7,11},{8,4},{9,5},... | collective-permute-start | bytes 221192 | tf_op jit(solution)/shard_map/ppermute | solution.py:11
  27.4 6.2 %collective-permute-start.5 = (bf16[1,16,2304]{2,1,0:T(8,128)(2,1)S(1)}, bf16[1,16,2304]{2,1,0:T(8,128)(2,1)S(1)}, u32[]{:S(2)}, u32[]{:S(2)}) collective-permute-start(bf16[1,16,2304]{2,1,0:T(8,128)(2,1)S(1)} %get-tuple-element.17), channel_id=1, source_target_pairs={{0,12},{1,13},{2,14},{3,15},{4,8},{5,9},{6,10},{7,11},{8,4},{9,5},... | collective-permute-start | bytes 221192 | tf_op jit(solution)/shard_map/ppermute | solution.py:11
  30.2 6.8 %collective-permute-start.4 = (bf16[2,16,2304]{2,1,0:T(8,128)(2,1)S(1)}, bf16[2,16,2304]{2,1,0:T(8,128)(2,1)S(1)}, u32[]{:S(2)}, u32[]{:S(2)}) collective-permute-start(bf16[2,16,2304]{2,1,0:T(8,128)(2,1)S(1)} %pad_maximum_fusion.9), channel_id=1, source_target_pairs={{0,2},{1,3},{2,0},{3,1},{4,6},{5,7},{6,4},{7,5},{8,10},{9,11},{10,... | collective-permute-start | bytes 442376 | tf_op jit(solution)/shard_map/ppermute | solution.py:11
  33.6 5.2 %collective-permute-start.6 = (bf16[2,16,2304]{2,1,0:T(8,128)(2,1)S(1)}, bf16[2,16,2304]{2,1,0:T(8,128)(2,1)S(1)}, u32[]{:S(2)}, u32[]{:S(2)}) collective-permute-start(bf16[2,16,2304]{2,1,0:T(8,128)(2,1)S(1)} %pad_maximum_fusion.10), channel_id=1, source_target_pairs={{0,4},{1,5},{2,6},{3,7},{4,0},{5,1},{6,2},{7,3},{8,12},{9,13},{10,... | collective-permute-start | bytes 442376 | tf_op jit(solution)/shard_map/ppermute | solution.py:11
  38.9 6.8 %collective-permute-start.8 = (bf16[4,16,2304]{2,1,0:T(8,128)(2,1)S(1)}, bf16[4,16,2304]{2,1,0:T(8,128)(2,1)S(1)}, u32[]{:S(2)}, u32[]{:S(2)}) collective-permute-start(bf16[4,16,2304]{2,1,0:T(8,128)(2,1)S(1)} %pad_maximum_fusion.7), channel_id=1, source_target_pairs={{0,2},{1,3},{2,0},{3,1},{4,6},{5,7},{6,4},{7,5},{8,10},{9,11},{10,... | collective-permute-start | bytes 884744 | tf_op jit(solution)/shard_map/ppermute | solution.py:11
  40.4 6.8 %collective-permute-start.7 = (bf16[4,16,2304]{2,1,0:T(8,128)(2,1)S(1)}, bf16[4,16,2304]{2,1,0:T(8,128)(2,1)S(1)}, u32[]{:S(2)}, u32[]{:S(2)}) collective-permute-start(bf16[4,16,2304]{2,1,0:T(8,128)(2,1)S(1)} %pad_maximum_fusion.6), channel_id=1, source_target_pairs={{0,4},{1,5},{2,6},{3,7},{4,0},{5,1},{6,2},{7,3},{8,12},{9,13},{10,... | collective-permute-start | bytes 884744 | tf_op jit(solution)/shard_map/ppermute | solution.py:11
  47.8 1.4 %copy-start.4 = (s32[256]{0:T(256)S(1)}, s32[256]{0:T(256)}, u32[]{:S(2)}) copy-start(s32[256]{0:T(256)} %table.5) | copy-start | bytes 3076
  48.3 3.5 %collective-permute-start.9 = (bf16[128,256]{1,0:T(8,128)(2,1)S(1)}, bf16[128,256]{1,0:T(8,128)(2,1)S(1)}, u32[]{:S(2)}, u32[]{:S(2)}) collective-permute-start(bf16[128,256]{1,0:T(8,128)(2,1)S(1)} %pad_maximum_fusion.12), channel_id=1, source_target_pairs={{0,1},{1,0},{2,3},{3,2},{4,5},{5,4},{6,7},{7,6},{8,9},{9,8},{10,11... | collective-permute-start | bytes 196616 | tf_op jit(solution)/shard_map/ppermute | solution.py:11
  51.7 1.3 %copy-start.7 = (bf16[1,128,4608]{2,1,0:T(8,128)(2,1)S(1)}, bf16[1,128,4608]{2,1,0:T(8,128)(2,1)}, u32[]{:S(2)}) copy-start(bf16[1,128,4608]{2,1,0:T(8,128)(2,1)} %param.20) | copy-start | bytes 3538948
  53.4 5.3 %copy-start.8 = (f32[128,2304]{1,0:T(8,128)}, f32[128,2304]{1,0:T(8,128)S(1)}, u32[]{:S(2)}) copy-start(f32[128,2304]{1,0:T(8,128)S(1)} %fusion.6) | copy-start | bytes 3538948
  54.2 9.7 %collective-permute-start.11 = (bf16[4,16,2304]{2,1,0:T(8,128)(2,1)}, bf16[4,16,2304]{2,1,0:T(8,128)(2,1)}, u32[]{:S(2)}, u32[]{:S(2)}) collective-permute-start(bf16[4,16,2304]{2,1,0:T(8,128)(2,1)} %bitcast.21), channel_id=1, source_target_pairs={{0,4},{1,5},{2,6},{3,7},{4,0},{5,1},{6,2},{7,3},{8,12},{9,13},{10,... | collective-permute-start | bytes 884744 | tf_op jit(solution)/shard_map/ppermute | solution.py:11
  58.7 5.2 %slice-start = ((f32[128,2304]{1,0:T(8,128)}), f32[64,2304]{1,0:T(8,128)S(1)}, s32[]{:S(2)}) async-start(f32[128,2304]{1,0:T(8,128)} %copy-done.8), calls=%async_computation.1 | async-start | bytes 1179648 | tf_op jit(solution)/shard_map/slice | solution.py:265
  58.8 9.9 %collective-permute-start.14 = (bf16[4,16,2304]{2,1,0:T(8,128)(2,1)S(1)}, bf16[4,16,2304]{2,1,0:T(8,128)(2,1)S(1)}, u32[]{:S(2)}, u32[]{:S(2)}) collective-permute-start(bf16[4,16,2304]{2,1,0:T(8,128)(2,1)S(1)} %bitcast.80), channel_id=1, source_target_pairs={{0,2},{1,3},{2,0},{3,1},{4,6},{5,7},{6,4},{7,5},{8,10},{9,11},{10,... | collective-permute-start | bytes 884744 | tf_op jit(solution)/shard_map/ppermute | solution.py:11
  64.9 6.2 %collective-permute-start.12 = (bf16[2,16,2304]{2,1,0:T(8,128)(2,1)S(1)}, bf16[2,16,2304]{2,1,0:T(8,128)(2,1)S(1)}, u32[]{:S(2)}, u32[]{:S(2)}) collective-permute-start(bf16[2,16,2304]{2,1,0:T(8,128)(2,1)S(1)} %slice.235), channel_id=1, source_target_pairs={{0,2},{1,3},{2,0},{3,1},{4,6},{5,7},{6,4},{7,5},{8,10},{9,11},{10,... | collective-permute-start | bytes 442376 | tf_op jit(solution)/shard_map/ppermute | solution.py:11
  68.8 5.2 %collective-permute-start.15 = (bf16[2,16,2304]{2,1,0:T(8,128)(2,1)S(1)}, bf16[2,16,2304]{2,1,0:T(8,128)(2,1)S(1)}, u32[]{:S(2)}, u32[]{:S(2)}) collective-permute-start(bf16[2,16,2304]{2,1,0:T(8,128)(2,1)S(1)} %slice.234), channel_id=1, source_target_pairs={{0,4},{1,5},{2,6},{3,7},{4,0},{5,1},{6,2},{7,3},{8,12},{9,13},{10,... | collective-permute-start | bytes 442376 | tf_op jit(solution)/shard_map/ppermute | solution.py:11
  71.2 9.3 %copy-start.10 = (bf16[16,4608]{1,0:T(8,128)(2,1)S(1)}, bf16[16,4608]{1,0:T(8,128)(2,1)}, u32[]{:S(2)}) copy-start(bf16[16,4608]{1,0:T(8,128)(2,1)} %copy-done.9) | copy-start | bytes 442372
  71.2 9.3 %copy-start.13 = (f32[4608]{0:T(1024)S(1)}, f32[4608]{0:T(1024)}, u32[]{:S(2)}) copy-start(f32[4608]{0:T(1024)} %reduce.1) | copy-start | bytes 55300
  71.2 6.3 %collective-permute-start.13 = (bf16[1,16,2304]{2,1,0:T(8,128)(2,1)S(1)}, bf16[1,16,2304]{2,1,0:T(8,128)(2,1)S(1)}, u32[]{:S(2)}, u32[]{:S(2)}) collective-permute-start(bf16[1,16,2304]{2,1,0:T(8,128)(2,1)S(1)} %slice.237), channel_id=1, source_target_pairs={{0,12},{1,13},{2,14},{3,15},{4,8},{5,9},{6,10},{7,11},{8,4},{9,5},... | collective-permute-start | bytes 221192 | tf_op jit(solution)/shard_map/ppermute | solution.py:11
  74.0 6.2 %collective-permute-start.16 = (bf16[1,16,2304]{2,1,0:T(8,128)(2,1)S(1)}, bf16[1,16,2304]{2,1,0:T(8,128)(2,1)S(1)}, u32[]{:S(2)}, u32[]{:S(2)}) collective-permute-start(bf16[1,16,2304]{2,1,0:T(8,128)(2,1)S(1)} %slice.236), channel_id=1, source_target_pairs={{0,12},{1,13},{2,14},{3,15},{4,8},{5,9},{6,10},{7,11},{8,4},{9,5},... | collective-permute-start | bytes 221192 | tf_op jit(solution)/shard_map/ppermute | solution.py:11
  (5 other events, 4.0 us)

commit v2 on v1

--- a/solution.py
+++ b/solution.py
@@ -205,14 +205,13 @@
     rest = rest[:-1] if len(rest) > 1 else []
     orders = [top + rest, top + rest[::-1]]
     normed = rms_norm(checked.astype(jnp.float32), pre_gain[0]).astype(jnp.bfloat16)
+    late_rank, late_gain, normed = lax.optimization_barrier((rank, post_gain, normed))
     cut = width // 256 * 128
     columns = [(0, cut), (cut, width)]
     layout = span(orders[0])
     parts = [normed[None, :, a:b] for a, b in columns]
     for stage in range(len(orders[0])):
         sent = [swap(part, "dp", order[stage]) for part, order in zip(parts, orders)]
-        if stage == 1:
-            weights, sent = lax.optimization_barrier((weights, sent))
         parts = [jnp.concatenate([part, got]) for part, got in zip(parts, sent)]
     rows = [part.reshape(-1, part.shape[-1]) for part in parts]
     half = rows[0].shape[0]
@@ -222,10 +221,10 @@
         for part, (a, b) in zip(rows, columns)
     ]
     proj = proj[0] + turn(proj[1], len(rest))
-    own_at = (rank ^ jnp.array(layout, dtype=jnp.int32)) * tokens
+    own_at = (late_rank ^ jnp.array(layout, dtype=jnp.int32)) * tokens
     inner = jnp.arange(tokens, dtype=jnp.int32)
     positions = (own_at[:, None] + inner[None, :]).reshape(-1)
-    other_at = (rank ^ jnp.array([m ^ 1 for m in layout], dtype=jnp.int32)) * tokens
+    other_at = (late_rank ^ jnp.array([m ^ 1 for m in layout], dtype=jnp.int32)) * tokens
     positions_other = (other_at[:, None] + inner[None, :]).reshape(-1)
     is_even = rank % 2 == 0
     q_own, kv_own, q_other, kv_other = (proj[:, i * head : (i + 1) * head] for i in range(4))
@@ -252,21 +251,32 @@
     attended = jnp.concatenate([attended[:half], attended[half:]], axis=1)
     w_out = jnp.concatenate([output_weight[0], wo_other], axis=0)
 
-    sums = []
-    for (a, b), source in zip(columns, [attended, turn(attended, len(rest))]):
-        part = jnp.dot(source, w_out[:, a:b], preferred_element_type=jnp.float32)
-        sums.append(part.reshape(-1, tokens, b - a))
+    sources = [attended, turn(attended, len(rest))]
+    going, staying = [], []
+    for (a, b), source in zip(columns, sources):
+        part = jnp.dot(source[half // 2 :], w_out[:, a:b], preferred_element_type=jnp.float32)
+        going.append(part.astype(jnp.bfloat16).reshape(-1, tokens, b - a))
+    for (a, b), source in zip(columns, sources):
+        part = jnp.dot(source[: half // 2], w_out[:, a:b], preferred_element_type=jnp.float32)
+        staying.append(part.reshape(-1, tokens, b - a))
     for stage in reversed(range(len(orders[0]))):
-        sent = [
-            swap(part[part.shape[0] // 2 :].astype(jnp.bfloat16), "dp", order[stage])
-            for part, order in zip(sums, orders)
-        ]
-        sums = [
-            part[: part.shape[0] // 2] + got.astype(jnp.float32) for part, got in zip(sums, sent)
-        ]
+        sent = [swap(part, "dp", order[stage]) for part, order in zip(going, orders)]
+        middle = staying[0].shape[0] // 2
+        if stage > 0:
+            going = [
+                (part[middle:] + got[middle:].astype(jnp.float32)).astype(jnp.bfloat16)
+                for part, got in zip(staying, sent)
+            ]
+            staying = [
+                part[:middle] + got[:middle].astype(jnp.float32)
+                for part, got in zip(staying, sent)
+            ]
+        else:
+            staying = [part + got.astype(jnp.float32) for part, got in zip(staying, sent)]
+    sums = staying
     new_accumulators = place_blocks(block_sources, rank, incoming)
     summed = jnp.concatenate([part[0] for part in sums], axis=-1)
-    check_out = (checked.astype(jnp.float32) + rms_norm(summed, post_gain[0])).astype(jnp.bfloat16)
+    check_out = (checked.astype(jnp.float32) + rms_norm(summed, late_gain[0])).astype(jnp.bfloat16)
     return (moved, new_accumulators, check_out[None, :, :])
 
 

time: 81.8 us -> 80.7 us (0.987)
  local copies, waits for them, and re-layouts: 8.74 us -> 5.08 us
  other arithmetic: 9.22 us -> 5.79 us
  starting transfers between devices: 27.6 us -> 30.4 us
  waiting for transfers between devices: 23.1 us -> 25 us
  matrix products: 2.16 us -> 3.65 us
    ppermute x17, starting transfers between devices: 21.6 us -> 24.4 us  [swap(): return lax.ppermute(value, axis, pairs)]
    ppermute x17, waiting for transfers between devices: 23.1 us -> 25 us  [swap(): return lax.ppermute(value, axis, pairs)]
    dot_general x2 -> x4, matrix products: 0.67 us -> 2.16 us  [the longest x2 1.48 us: step(): jnp.dot(source[half // 2:], w_out[:, a:b], preferred_element_type=jnp.flo...]
    concatenate x1, local copies, waits for them, and re-layouts: 1.58 us -> 0.11 us  [step(): attended = jnp.concatenate([attended[:half], attended[half:]], axis=1)]
    add x4 -> x0, other arithmetic: 1.14 us -> none  [step(): part[:part.shape[0] // 2] + got.astype(jnp.float32)]
    another operation x2, other arithmetic: 1.67 us -> 0.76 us  [step(): moved = jnp.stack([checked] + [slot(j) for j in range(1, sections)])]
    slice x9 -> x3, local copies, waits for them, and re-layouts: 0.94 us -> 0.08 us  [the longest x2 0.08 us: step(): part[middle:] + got[middle:].astype(jnp.float32)]
    transpose x2 -> x1, local copies, waits for them, and re-layouts: 0.86 us -> 0.02 us  [turn(): return bits.transpose(order).reshape(values.shape)]
  transfers between devices with their start and end apart: 18 -> 18, of which waited for: 11 -> 11; matrix products, arithmetic and copies ran while one was open for 17% -> 10% of each run, Pallas kernels for 6% -> 6%
where the time goes in v2:
time: 80.7 us; the launch traced here: 80.3 us
  starting transfers between devices  30.4 us (38%)
  waiting for transfers between devices  25 us (31%)
  other arithmetic  5.79 us (7%)
  Pallas kernels  5.44 us (7%)
  local copies, waits for them, and re-layouts  5.08 us (6%)
  between operations  4.95 us (6%)
  matrix products  3.65 us (5%)
    ppermute x17, waiting for transfers between devices, swap(): return lax.ppermute(value, axis, pairs)  25 us
    ppermute x17, starting transfers between devices, swap(): return lax.ppermute(value, axis, pairs)  24.4 us
    all_to_all x1, starting transfers between devices, step(): lax.all_to_all(outgoing, 'dp', split_axis=0, concat_axis=0, tiled=True)  6.05 us
    unnamed x28, local copies, waits for them, and re-layouts  3.97 us
    pallas_call x1, Pallas kernels, place_blocks(): pl.pallas_call(body, out_shape=jax.ShapeDtypeStruct((groups, rows, width)...  2.62 us
    pallas_call x1, Pallas kernels, pack_blocks(): pl.pallas_call(body, out_shape=jax.ShapeDtypeStruct((groups, rows, width...  2.07 us
    concatenate x1, other arithmetic, step(): jnp.concatenate([query_weight[0], keyval_weight[0], wq_other, wkv_other],...  1.9 us
  transfers between devices with their start and end apart: 18, of which 11 were waited for; matrix products, arithmetic and copies ran while one was open for 10% of the time, Pallas kernels for 6%

profile of v2, /device:TPU:0, one launch (start us, length us, event | category | flops | bytes accessed | tf_op | source)
XLA Modules:
  0.0 80.3 jit_solution(13687784567342423867)
XLA Ops:
  0.7 1.0 %copy-done = bf16[2,16,4608]{2,1,0:T(8,128)(2,1)S(1)} copy-done((bf16[2,16,4608]{2,1,0:T(8,128)(2,1)S(1)}, bf16[2,16,4608]{2,1,0:T(8,128)(2,1)}, u32[]{:S(2)}) %copy-start) | copy-done | bytes 294936
  2.3 0.7 pick_sends.1
  3.0 3.0 %collective-permute-start = (bf16[16,4608]{1,0:T(8,128)(2,1)S(1)}, bf16[16,4608]{1,0:T(8,128)(2,1)S(1)}, u32[]{:S(2)}, u32[]{:S(2)}) collective-permute-start(bf16[16,4608]{1,0:T(8,128)(2,1)S(1)} %bitcast.71), channel_id=1, source_target_pairs={{0,16},{16,0},{1,17},{17,1},{2,18},{18,2},{3,19},{19,3},{4,20},{20... | collective-permute-start | bytes 442376 | tf_op jit(solution)/shard_map/ppermute | solution.py:11
  7.2 1.1 %copy-done.2 = f32[16,2,4608]{2,1,0:T(2,128)S(1)} copy-done((f32[16,2,4608]{2,1,0:T(2,128)S(1)}, f32[16,2,4608]{2,1,0:T(2,128)}, u32[]{:S(2)}) %copy-start.2) | copy-done | bytes 589848
  8.3 0.7 copy-done.3
  9.0 2.1 %pack_blocks.1 = bf16[16,2,4736]{2,1,0:T(2,128)(2,1)} custom-call(s32[256]{0:T(256)S(1)} %copy-done.3, s32[1]{0:T(128)} %bitcast.8.own_ref, f32[16,2,4608]{2,1,0:T(2,128)S(1)} %copy-done.2, f32[1,1]{1,0:T(1,128)S(6)} %copy.19.term_ref), custom_call_target="tpu_custom_call" | custom-call | tf_op jit(solution)/shard_map/pack_blocks/pallas_call | solution.py:93
  11.0 6.0 %all-to-all-start = ((bf16[16,2,4736]{2,1,0:T(2,128)(2,1)}), bf16[16,2,4736]{2,1,0:T(2,128)(2,1)S(1)}, u32[]{:S(2)}, u32[]{:S(2)}) async-start(bf16[16,2,4736]{2,1,0:T(2,128)(2,1)} %pack_blocks.1), calls=%async_computation | async-start | bytes 606208 | tf_op jit(solution)/shard_map/all_to_all | solution.py:185
  22.2 3.8 %collective-permute-start.1 = (bf16[1,16,2304]{2,1,0:T(8,128)(2,1)S(1)}, bf16[1,16,2304]{2,1,0:T(8,128)(2,1)S(1)}, u32[]{:S(2)}, u32[]{:S(2)}) collective-permute-start(bf16[1,16,2304]{2,1,0:T(8,128)(2,1)S(1)} %get-tuple-element.25), channel_id=1, source_target_pairs={{0,12},{1,13},{2,14},{3,15},{4,8},{5,9},{6,10},{7,11},{8,4},{9,5},... | collective-permute-start | bytes 221192 | tf_op jit(solution)/shard_map/ppermute | solution.py:11
  26.2 0.7 pad_maximum_fusion.4
  27.2 1.5 %collective-permute-done.1 = bf16[1,16,2304]{2,1,0:T(8,128)(2,1)S(1)} collective-permute-done((bf16[1,16,2304]{2,1,0:T(8,128)(2,1)S(1)}, bf16[1,16,2304]{2,1,0:T(8,128)(2,1)S(1)}, u32[]{:S(2)}, u32[]{:S(2)}) %collective-permute-start.1) | collective-permute-done | bytes 73760 | tf_op jit(solution)/shard_map/ppermute | solution.py:11
  28.7 1.7 %collective-permute-start.2 = (bf16[2,16,2304]{2,1,0:T(8,128)(2,1)S(1)}, bf16[2,16,2304]{2,1,0:T(8,128)(2,1)S(1)}, u32[]{:S(2)}, u32[]{:S(2)}) collective-permute-start(bf16[2,16,2304]{2,1,0:T(8,128)(2,1)S(1)} %pad_maximum_fusion.10), channel_id=1, source_target_pairs={{0,2},{1,3},{2,0},{3,1},{4,6},{5,7},{6,4},{7,5},{8,10},{9,11},{10,... | collective-permute-start | bytes 442376 | tf_op jit(solution)/shard_map/ppermute | solution.py:11
  30.4 1.7 %collective-permute-done.6 = bf16[1,16,2304]{2,1,0:T(8,128)(2,1)S(1)} collective-permute-done((bf16[1,16,2304]{2,1,0:T(8,128)(2,1)S(1)}, bf16[1,16,2304]{2,1,0:T(8,128)(2,1)S(1)}, u32[]{:S(2)}, u32[]{:S(2)}) %collective-permute-start.6) | collective-permute-done | bytes 73760 | tf_op jit(solution)/shard_map/ppermute | solution.py:11
  32.1 3.0 %collective-permute-start.7 = (bf16[2,16,2304]{2,1,0:T(8,128)(2,1)S(1)}, bf16[2,16,2304]{2,1,0:T(8,128)(2,1)S(1)}, u32[]{:S(2)}, u32[]{:S(2)}) collective-permute-start(bf16[2,16,2304]{2,1,0:T(8,128)(2,1)S(1)} %pad_maximum_fusion.11), channel_id=1, source_target_pairs={{0,4},{1,5},{2,6},{3,7},{4,0},{5,1},{6,2},{7,3},{8,12},{9,13},{10,... | collective-permute-start | bytes 442376 | tf_op jit(solution)/shard_map/ppermute | solution.py:11
  35.1 3.7 %collective-permute-start.3 = (bf16[4,16,2304]{2,1,0:T(8,128)(2,1)S(1)}, bf16[4,16,2304]{2,1,0:T(8,128)(2,1)S(1)}, u32[]{:S(2)}, u32[]{:S(2)}) collective-permute-start(bf16[4,16,2304]{2,1,0:T(8,128)(2,1)S(1)} %pad_maximum_fusion.5), channel_id=1, source_target_pairs={{0,4},{1,5},{2,6},{3,7},{4,0},{5,1},{6,2},{7,3},{8,12},{9,13},{10,... | collective-permute-start | bytes 884744 | tf_op jit(solution)/shard_map/ppermute | solution.py:11
  38.8 1.0 %collective-permute-done.7 = bf16[2,16,2304]{2,1,0:T(8,128)(2,1)S(1)} collective-permute-done((bf16[2,16,2304]{2,1,0:T(8,128)(2,1)S(1)}, bf16[2,16,2304]{2,1,0:T(8,128)(2,1)S(1)}, u32[]{:S(2)}, u32[]{:S(2)}) %collective-permute-start.7) | collective-permute-done | bytes 147488 | tf_op jit(solution)/shard_map/ppermute | solution.py:11
  39.9 1.0 %collective-permute-start.8 = (bf16[4,16,2304]{2,1,0:T(8,128)(2,1)S(1)}, bf16[4,16,2304]{2,1,0:T(8,128)(2,1)S(1)}, u32[]{:S(2)}, u32[]{:S(2)}) collective-permute-start(bf16[4,16,2304]{2,1,0:T(8,128)(2,1)S(1)} %pad_maximum_fusion.6), channel_id=1, source_target_pairs={{0,2},{1,3},{2,0},{3,1},{4,6},{5,7},{6,4},{7,5},{8,10},{9,11},{10,... | collective-permute-start | bytes 884744 | tf_op jit(solution)/shard_map/ppermute | solution.py:11
  40.8 3.6 %collective-permute-done.3 = bf16[4,16,2304]{2,1,0:T(8,128)(2,1)S(1)} collective-permute-done((bf16[4,16,2304]{2,1,0:T(8,128)(2,1)S(1)}, bf16[4,16,2304]{2,1,0:T(8,128)(2,1)S(1)}, u32[]{:S(2)}, u32[]{:S(2)}) %collective-permute-start.3) | collective-permute-done | bytes 294944 | tf_op jit(solution)/shard_map/ppermute | solution.py:11
  44.5 2.2 %collective-permute-done.8 = bf16[4,16,2304]{2,1,0:T(8,128)(2,1)S(1)} collective-permute-done((bf16[4,16,2304]{2,1,0:T(8,128)(2,1)S(1)}, bf16[4,16,2304]{2,1,0:T(8,128)(2,1)S(1)}, u32[]{:S(2)}, u32[]{:S(2)}) %collective-permute-start.8) | collective-permute-done | bytes 294944 | tf_op jit(solution)/shard_map/ppermute | solution.py:11
  46.8 1.9 %pad_maximum_fusion = bf16[4608,512]{1,0:T(8,128)(2,1)S(1)} fusion(bf16[4608,128]{1,0:T(8,128)(2,1)} %collective-permute-done.5, bf16[4608,128]{1,0:T(8,128)(2,1)} %collective-permute-done.4, bf16[4608,128]{1,0:T(8,128)(2,1)S(1)} %bitcast.79, bf16[4608,128]{1,0:T(8,128)(2,1)S(1)} %bitcast.81), kind=kLoop, calls=%fused_computation | loop fusion | flops 18874368 | bytes 9437184 | tf_op jit(solution)/shard_map/concatenate | solution.py:199
  50.3 2.6 %place_blocks.1 = f32[16,2,4608]{2,1,0:T(2,128)} custom-call(s32[256]{0:T(256)S(1)} %copy-done.4, s32[1]{0:T(128)} %bitcast.8.own_ref, bf16[16,2,4736]{2,1,0:T(2,128)(2,1)S(1)} %all-to-all-done.held), custom_call_target="tpu_custom_call" | custom-call | tf_op jit(solution)/shard_map/place_blocks/pallas_call | solution.py:128
  54.2 1.1 %convolution_convert_fusion.1 = bf16[64,2304]{1,0:T(8,128)(2,1)} fusion(bf16[128,128]{0,1:T(8,128)(2,1)S(1)} %get-tuple-element.31, bf16[128,128]{0,1:T(8,128)(2,1)S(1)} %get-tuple-element.32, bf16[128,4608]{1,0:T(8,128)(2,1)S(1)} %bitcast.73, bf16[128,4608]{1,0:T(8,128)(2,1)S(1)} %collective-permute-done.10), kind=kOutput, calls=%fused_computation.2 | convolution fusion | flops 78069760 | bytes 2719744 | tf_op jit(solution)/shard_map/dot_general | solution.py:257
  55.3 2.0 %collective-permute-start.11 = (bf16[4,16,2304]{2,1,0:T(8,128)(2,1)}, bf16[4,16,2304]{2,1,0:T(8,128)(2,1)S(1)}, u32[]{:S(2)}, u32[]{:S(2)}) collective-permute-start(bf16[4,16,2304]{2,1,0:T(8,128)(2,1)} %bitcast.21), channel_id=1, source_target_pairs={{0,4},{1,5},{2,6},{3,7},{4,0},{5,1},{6,2},{7,3},{8,12},{9,13},{10,... | collective-permute-start | bytes 884744 | tf_op jit(solution)/shard_map/ppermute | solution.py:11
  58.6 1.0 %collective-permute-start.14 = (bf16[4,16,2304]{2,1,0:T(8,128)(2,1)S(1)}, bf16[4,16,2304]{2,1,0:T(8,128)(2,1)S(1)}, u32[]{:S(2)}, u32[]{:S(2)}) collective-permute-start(bf16[4,16,2304]{2,1,0:T(8,128)(2,1)S(1)} %bitcast.88), channel_id=1, source_target_pairs={{0,2},{1,3},{2,0},{3,1},{4,6},{5,7},{6,4},{7,5},{8,10},{9,11},{10,... | collective-permute-start | bytes 884744 | tf_op jit(solution)/shard_map/ppermute | solution.py:11
  59.5 5.7 %collective-permute-done.11 = bf16[4,16,2304]{2,1,0:T(8,128)(2,1)S(1)} collective-permute-done((bf16[4,16,2304]{2,1,0:T(8,128)(2,1)}, bf16[4,16,2304]{2,1,0:T(8,128)(2,1)S(1)}, u32[]{:S(2)}, u32[]{:S(2)}) %collective-permute-start.11) | collective-permute-done | bytes 294944 | tf_op jit(solution)/shard_map/ppermute | solution.py:11
  65.2 1.0 %collective-permute-start.12 = (bf16[2,16,2304]{2,1,0:T(8,128)(2,1)S(1)}, bf16[2,16,2304]{2,1,0:T(8,128)(2,1)S(1)}, u32[]{:S(2)}, u32[]{:S(2)}) collective-permute-start(bf16[2,16,2304]{2,1,0:T(8,128)(2,1)S(1)} %get-tuple-element.17), channel_id=1, source_target_pairs={{0,2},{1,3},{2,0},{3,1},{4,6},{5,7},{6,4},{7,5},{8,10},{9,11},{10,... | collective-permute-start | bytes 442376 | tf_op jit(solution)/shard_map/ppermute | solution.py:11
  66.2 1.5 %collective-permute-done.14 = bf16[4,16,2304]{2,1,0:T(8,128)(2,1)S(1)} collective-permute-done((bf16[4,16,2304]{2,1,0:T(8,128)(2,1)S(1)}, bf16[4,16,2304]{2,1,0:T(8,128)(2,1)S(1)}, u32[]{:S(2)}, u32[]{:S(2)}) %collective-permute-start.14) | collective-permute-done | bytes 294944 | tf_op jit(solution)/shard_map/ppermute | solution.py:11
  68.1 2.8 %collective-permute-done.12 = bf16[2,16,2304]{2,1,0:T(8,128)(2,1)S(1)} collective-permute-done((bf16[2,16,2304]{2,1,0:T(8,128)(2,1)S(1)}, bf16[2,16,2304]{2,1,0:T(8,128)(2,1)S(1)}, u32[]{:S(2)}, u32[]{:S(2)}) %collective-permute-start.12) | collective-permute-done | bytes 147488 | tf_op jit(solution)/shard_map/ppermute | solution.py:11
  71.0 1.4 %collective-permute-start.13 = (bf16[1,16,2304]{2,1,0:T(8,128)(2,1)S(1)}, bf16[1,16,2304]{2,1,0:T(8,128)(2,1)S(1)}, u32[]{:S(2)}, u32[]{:S(2)}) collective-permute-start(bf16[1,16,2304]{2,1,0:T(8,128)(2,1)S(1)} %fusion.22), channel_id=1, source_target_pairs={{0,12},{1,13},{2,14},{3,15},{4,8},{5,9},{6,10},{7,11},{8,4},{9,5},... | collective-permute-start | bytes 221192 | tf_op jit(solution)/shard_map/ppermute | solution.py:11
  73.0 1.9 %collective-permute-start.16 = (bf16[1,16,2304]{2,1,0:T(8,128)(2,1)S(1)}, bf16[1,16,2304]{2,1,0:T(8,128)(2,1)S(1)}, u32[]{:S(2)}, u32[]{:S(2)}) collective-permute-start(bf16[1,16,2304]{2,1,0:T(8,128)(2,1)S(1)} %fusion.19), channel_id=1, source_target_pairs={{0,12},{1,13},{2,14},{3,15},{4,8},{5,9},{6,10},{7,11},{8,4},{9,5},... | collective-permute-start | bytes 221192 | tf_op jit(solution)/shard_map/ppermute | solution.py:11
  75.0 2.3 %collective-permute-done.13 = bf16[1,16,2304]{2,1,0:T(8,128)(2,1)S(1)} collective-permute-done((bf16[1,16,2304]{2,1,0:T(8,128)(2,1)S(1)}, bf16[1,16,2304]{2,1,0:T(8,128)(2,1)S(1)}, u32[]{:S(2)}, u32[]{:S(2)}) %collective-permute-start.13) | collective-permute-done | bytes 73760 | tf_op jit(solution)/shard_map/ppermute | solution.py:11
  77.3 2.1 %collective-permute-done.16 = bf16[1,16,2304]{2,1,0:T(8,128)(2,1)S(1)} collective-permute-done((bf16[1,16,2304]{2,1,0:T(8,128)(2,1)S(1)}, bf16[1,16,2304]{2,1,0:T(8,128)(2,1)S(1)}, u32[]{:S(2)}, u32[]{:S(2)}) %collective-permute-start.16) | collective-permute-done | bytes 73760 | tf_op jit(solution)/shard_map/ppermute | solution.py:11
  79.5 0.8 fusion.18
  (90 shorter events, 9.0 us)
Async XLA Ops:
  0.6 16.5 %copy-start.6 = (s32[4]{0:T(128)S(1)}, s32[4]{0:T(128)}, u32[]{:S(2)}) copy-start(s32[4]{0:T(128)} %table.3) | copy-start | bytes 52
  0.6 1.0 %copy-start = (bf16[2,16,4608]{2,1,0:T(8,128)(2,1)S(1)}, bf16[2,16,4608]{2,1,0:T(8,128)(2,1)}, u32[]{:S(2)}) copy-start(bf16[2,16,4608]{2,1,0:T(8,128)(2,1)} %held.2) | copy-start | bytes 884740
  1.6 0.7 copy-start.5
  2.3 19.5 %copy-start.10 = (f32[1,4608]{1,0:T(1,128)S(1)}, f32[1,4608]{1,0:T(1,128)}, u32[]{:S(2)}) copy-start(f32[1,4608]{1,0:T(1,128)} %param.17) | copy-start | bytes 55300
  2.3 19.6 %copy-start.1 = (bf16[2,16,4608]{2,1,0:T(8,128)(2,1)S(1)}, bf16[2,16,4608]{2,1,0:T(8,128)(2,1)}, u32[]{:S(2)}) copy-start(bf16[2,16,4608]{2,1,0:T(8,128)(2,1)} %held.2) | copy-start | bytes 884740
  3.0 18.8 %collective-permute-start = (bf16[16,4608]{1,0:T(8,128)(2,1)S(1)}, bf16[16,4608]{1,0:T(8,128)(2,1)S(1)}, u32[]{:S(2)}, u32[]{:S(2)}) collective-permute-start(bf16[16,4608]{1,0:T(8,128)(2,1)S(1)} %bitcast.71), channel_id=1, source_target_pairs={{0,16},{16,0},{1,17},{17,1},{2,18},{18,2},{3,19},{19,3},{4,20},{20... | collective-permute-start | bytes 442376 | tf_op jit(solution)/shard_map/ppermute | solution.py:11
  6.1 40.7 %collective-permute-start.4 = (bf16[4608,128]{1,0:T(8,128)(2,1)}, bf16[4608,128]{1,0:T(8,128)(2,1)}, u32[]{:S(2)}, u32[]{:S(2)}) collective-permute-start(bf16[4608,128]{1,0:T(8,128)(2,1)} %bitcast.80), channel_id=1, source_target_pairs={{0,1},{1,0},{2,3},{3,2},{4,5},{5,4},{6,7},{7,6},{8,9},{9,8},{10,11... | collective-permute-start | bytes 3538952 | tf_op jit(solution)/shard_map/ppermute | solution.py:11
  6.1 40.7 %collective-permute-start.5 = (bf16[4608,128]{1,0:T(8,128)(2,1)}, bf16[4608,128]{1,0:T(8,128)(2,1)}, u32[]{:S(2)}, u32[]{:S(2)}) collective-permute-start(bf16[4608,128]{1,0:T(8,128)(2,1)} %bitcast.78), channel_id=1, source_target_pairs={{0,1},{1,0},{2,3},{3,2},{4,5},{5,4},{6,7},{7,6},{8,9},{9,8},{10,11... | collective-permute-start | bytes 3538952 | tf_op jit(solution)/shard_map/ppermute | solution.py:11
  6.6 47.0 %collective-permute-start.10 = (bf16[128,4608]{1,0:T(8,128)(2,1)}, bf16[128,4608]{1,0:T(8,128)(2,1)S(1)}, u32[]{:S(2)}, u32[]{:S(2)}) collective-permute-start(bf16[128,4608]{1,0:T(8,128)(2,1)} %bitcast.72), channel_id=1, source_target_pairs={{0,1},{1,0},{2,3},{3,2},{4,5},{5,4},{6,7},{7,6},{8,9},{9,8},{10,11... | collective-permute-start | bytes 3538952 | tf_op jit(solution)/shard_map/ppermute | solution.py:11
  7.2 1.1 %copy-start.2 = (f32[16,2,4608]{2,1,0:T(2,128)S(1)}, f32[16,2,4608]{2,1,0:T(2,128)}, u32[]{:S(2)}) copy-start(f32[16,2,4608]{2,1,0:T(2,128)} %held.3) | copy-start | bytes 1769476
  8.3 0.7 copy-start.3
  9.0 17.1 %copy-start.12 = (s32[8]{0:T(128)S(1)}, s32[8]{0:T(128)}, u32[]{:S(2)}) copy-start(s32[8]{0:T(128)} %constant.74.clone) | copy-start | bytes 100
  9.0 17.1 %copy-start.13 = (s32[8]{0:T(128)S(1)}, s32[8]{0:T(128)}, u32[]{:S(2)}) copy-start(s32[8]{0:T(128)} %constant.75.clone) | copy-start | bytes 100
  11.0 39.2 %all-to-all-start = ((bf16[16,2,4736]{2,1,0:T(2,128)(2,1)}), bf16[16,2,4736]{2,1,0:T(2,128)(2,1)S(1)}, u32[]{:S(2)}, u32[]{:S(2)}) async-start(bf16[16,2,4736]{2,1,0:T(2,128)(2,1)} %pack_blocks.1), calls=%async_computation | async-start | bytes 606208 | tf_op jit(solution)/shard_map/all_to_all | solution.py:185
  17.1 10.0 %copy-start.11 = (f32[1,4608]{1,0:T(1,128)S(1)}, f32[1,4608]{1,0:T(1,128)}, u32[]{:S(2)}) copy-start(f32[1,4608]{1,0:T(1,128)} %param.21) | copy-start | bytes 55300
  22.2 6.5 %collective-permute-start.1 = (bf16[1,16,2304]{2,1,0:T(8,128)(2,1)S(1)}, bf16[1,16,2304]{2,1,0:T(8,128)(2,1)S(1)}, u32[]{:S(2)}, u32[]{:S(2)}) collective-permute-start(bf16[1,16,2304]{2,1,0:T(8,128)(2,1)S(1)} %get-tuple-element.25), channel_id=1, source_target_pairs={{0,12},{1,13},{2,14},{3,15},{4,8},{5,9},{6,10},{7,11},{8,4},{9,5},... | collective-permute-start | bytes 221192 | tf_op jit(solution)/shard_map/ppermute | solution.py:11
  26.0 6.2 %collective-permute-start.6 = (bf16[1,16,2304]{2,1,0:T(8,128)(2,1)S(1)}, bf16[1,16,2304]{2,1,0:T(8,128)(2,1)S(1)}, u32[]{:S(2)}, u32[]{:S(2)}) collective-permute-start(bf16[1,16,2304]{2,1,0:T(8,128)(2,1)S(1)} %get-tuple-element.26), channel_id=1, source_target_pairs={{0,12},{1,13},{2,14},{3,15},{4,8},{5,9},{6,10},{7,11},{8,4},{9,5},... | collective-permute-start | bytes 221192 | tf_op jit(solution)/shard_map/ppermute | solution.py:11
  28.7 6.4 %collective-permute-start.2 = (bf16[2,16,2304]{2,1,0:T(8,128)(2,1)S(1)}, bf16[2,16,2304]{2,1,0:T(8,128)(2,1)S(1)}, u32[]{:S(2)}, u32[]{:S(2)}) collective-permute-start(bf16[2,16,2304]{2,1,0:T(8,128)(2,1)S(1)} %pad_maximum_fusion.10), channel_id=1, source_target_pairs={{0,2},{1,3},{2,0},{3,1},{4,6},{5,7},{6,4},{7,5},{8,10},{9,11},{10,... | collective-permute-start | bytes 442376 | tf_op jit(solution)/shard_map/ppermute | solution.py:11
  32.1 7.7 %collective-permute-start.7 = (bf16[2,16,2304]{2,1,0:T(8,128)(2,1)S(1)}, bf16[2,16,2304]{2,1,0:T(8,128)(2,1)S(1)}, u32[]{:S(2)}, u32[]{:S(2)}) collective-permute-start(bf16[2,16,2304]{2,1,0:T(8,128)(2,1)S(1)} %pad_maximum_fusion.11), channel_id=1, source_target_pairs={{0,4},{1,5},{2,6},{3,7},{4,0},{5,1},{6,2},{7,3},{8,12},{9,13},{10,... | collective-permute-start | bytes 442376 | tf_op jit(solution)/shard_map/ppermute | solution.py:11
  35.1 9.3 %collective-permute-start.3 = (bf16[4,16,2304]{2,1,0:T(8,128)(2,1)S(1)}, bf16[4,16,2304]{2,1,0:T(8,128)(2,1)S(1)}, u32[]{:S(2)}, u32[]{:S(2)}) collective-permute-start(bf16[4,16,2304]{2,1,0:T(8,128)(2,1)S(1)} %pad_maximum_fusion.5), channel_id=1, source_target_pairs={{0,4},{1,5},{2,6},{3,7},{4,0},{5,1},{6,2},{7,3},{8,12},{9,13},{10,... | collective-permute-start | bytes 884744 | tf_op jit(solution)/shard_map/ppermute | solution.py:11
  39.8 6.9 %copy-start.8 = (bf16[1,4608,128]{2,1,0:T(8,128)(2,1)S(1)}, bf16[1,4608,128]{2,1,0:T(8,128)(2,1)}, u32[]{:S(2)}) copy-start(bf16[1,4608,128]{2,1,0:T(8,128)(2,1)} %param.19) | copy-start | bytes 3538948
  39.8 6.9 %copy-start.9 = (bf16[1,4608,128]{2,1,0:T(8,128)(2,1)S(1)}, bf16[1,4608,128]{2,1,0:T(8,128)(2,1)}, u32[]{:S(2)}) copy-start(bf16[1,4608,128]{2,1,0:T(8,128)(2,1)} %param.18) | copy-start | bytes 3538948
  39.9 6.8 %collective-permute-start.8 = (bf16[4,16,2304]{2,1,0:T(8,128)(2,1)S(1)}, bf16[4,16,2304]{2,1,0:T(8,128)(2,1)S(1)}, u32[]{:S(2)}, u32[]{:S(2)}) collective-permute-start(bf16[4,16,2304]{2,1,0:T(8,128)(2,1)S(1)} %pad_maximum_fusion.6), channel_id=1, source_target_pairs={{0,2},{1,3},{2,0},{3,1},{4,6},{5,7},{6,4},{7,5},{8,10},{9,11},{10,... | collective-permute-start | bytes 884744 | tf_op jit(solution)/shard_map/ppermute | solution.py:11
  49.2 1.1 %copy-start.4 = (s32[256]{0:T(256)S(1)}, s32[256]{0:T(256)}, u32[]{:S(2)}) copy-start(s32[256]{0:T(256)} %table.5) | copy-start | bytes 3076
  50.2 2.7 %collective-permute-start.9 = (bf16[128,256]{1,0:T(8,128)(2,1)S(1)}, bf16[128,256]{1,0:T(8,128)(2,1)S(1)}, u32[]{:S(2)}, u32[]{:S(2)}) collective-permute-start(bf16[128,256]{1,0:T(8,128)(2,1)S(1)} %pad_maximum_fusion.14), channel_id=1, source_target_pairs={{0,1},{1,0},{2,3},{3,2},{4,5},{5,4},{6,7},{7,6},{8,9},{9,8},{10,11... | collective-permute-start | bytes 196616 | tf_op jit(solution)/shard_map/ppermute | solution.py:11
  52.9 1.3 %copy-start.7 = (bf16[1,128,4608]{2,1,0:T(8,128)(2,1)S(1)}, bf16[1,128,4608]{2,1,0:T(8,128)(2,1)}, u32[]{:S(2)}) copy-start(bf16[1,128,4608]{2,1,0:T(8,128)(2,1)} %param.20) | copy-start | bytes 3538948
  55.3 9.9 %collective-permute-start.11 = (bf16[4,16,2304]{2,1,0:T(8,128)(2,1)}, bf16[4,16,2304]{2,1,0:T(8,128)(2,1)S(1)}, u32[]{:S(2)}, u32[]{:S(2)}) collective-permute-start(bf16[4,16,2304]{2,1,0:T(8,128)(2,1)} %bitcast.21), channel_id=1, source_target_pairs={{0,4},{1,5},{2,6},{3,7},{4,0},{5,1},{6,2},{7,3},{8,12},{9,13},{10,... | collective-permute-start | bytes 884744 | tf_op jit(solution)/shard_map/ppermute | solution.py:11
  58.6 9.2 %collective-permute-start.14 = (bf16[4,16,2304]{2,1,0:T(8,128)(2,1)S(1)}, bf16[4,16,2304]{2,1,0:T(8,128)(2,1)S(1)}, u32[]{:S(2)}, u32[]{:S(2)}) collective-permute-start(bf16[4,16,2304]{2,1,0:T(8,128)(2,1)S(1)} %bitcast.88), channel_id=1, source_target_pairs={{0,2},{1,3},{2,0},{3,1},{4,6},{5,7},{6,4},{7,5},{8,10},{9,11},{10,... | collective-permute-start | bytes 884744 | tf_op jit(solution)/shard_map/ppermute | solution.py:11
  65.2 5.7 %collective-permute-start.12 = (bf16[2,16,2304]{2,1,0:T(8,128)(2,1)S(1)}, bf16[2,16,2304]{2,1,0:T(8,128)(2,1)S(1)}, u32[]{:S(2)}, u32[]{:S(2)}) collective-permute-start(bf16[2,16,2304]{2,1,0:T(8,128)(2,1)S(1)} %get-tuple-element.17), channel_id=1, source_target_pairs={{0,2},{1,3},{2,0},{3,1},{4,6},{5,7},{6,4},{7,5},{8,10},{9,11},{10,... | collective-permute-start | bytes 442376 | tf_op jit(solution)/shard_map/ppermute | solution.py:11
  67.8 5.2 %collective-permute-start.15 = (bf16[2,16,2304]{2,1,0:T(8,128)(2,1)S(1)}, bf16[2,16,2304]{2,1,0:T(8,128)(2,1)S(1)}, u32[]{:S(2)}, u32[]{:S(2)}) collective-permute-start(bf16[2,16,2304]{2,1,0:T(8,128)(2,1)S(1)} %get-tuple-element.19), channel_id=1, source_target_pairs={{0,4},{1,5},{2,6},{3,7},{4,0},{5,1},{6,2},{7,3},{8,12},{9,13},{10,... | collective-permute-start | bytes 442376 | tf_op jit(solution)/shard_map/ppermute | solution.py:11
  71.0 6.3 %collective-permute-start.13 = (bf16[1,16,2304]{2,1,0:T(8,128)(2,1)S(1)}, bf16[1,16,2304]{2,1,0:T(8,128)(2,1)S(1)}, u32[]{:S(2)}, u32[]{:S(2)}) collective-permute-start(bf16[1,16,2304]{2,1,0:T(8,128)(2,1)S(1)} %fusion.22), channel_id=1, source_target_pairs={{0,12},{1,13},{2,14},{3,15},{4,8},{5,9},{6,10},{7,11},{8,4},{9,5},... | collective-permute-start | bytes 221192 | tf_op jit(solution)/shard_map/ppermute | solution.py:11
  73.0 6.3 %collective-permute-start.16 = (bf16[1,16,2304]{2,1,0:T(8,128)(2,1)S(1)}, bf16[1,16,2304]{2,1,0:T(8,128)(2,1)S(1)}, u32[]{:S(2)}, u32[]{:S(2)}) collective-permute-start(bf16[1,16,2304]{2,1,0:T(8,128)(2,1)S(1)} %fusion.19), channel_id=1, source_target_pairs={{0,12},{1,13},{2,14},{3,15},{4,8},{5,9},{6,10},{7,11},{8,4},{9,5},... | collective-permute-start | bytes 221192 | tf_op jit(solution)/shard_map/ppermute | solution.py:11
